TPU v7x, 32 devices: a whole 2x2x4 slice. The times are simulated.
32 devices in a mesh: seq: 16 (over z, x, core), fsdp: 2 (over y).
Axes of the slice: x: 2, y: 2, z: 4, core: 2. Of those that a mesh axis runs over, the one named last changes fastest.
Arguments:
- hidden_next: bfloat16 [4096, 8192], P('seq'), may hold values from -6 to 6
- values_next: bfloat16 [4096, 8192], P('seq', 'fsdp'), may hold values from -6 to 6
- seg_next: int32 [4], replicated, may hold values from 1 to 2048, 4096 in all
- proj_bc: bfloat16 [8192, 1024], P(('seq', 'fsdp')), may hold values from -0.046875 to 0.046875
- proj_dt: bfloat16 [8192, 128], P(('seq', 'fsdp')), may hold values from -0.0625 to 0.0625
- dt_bias: float32 [128], replicated, may hold values from -4 to -2.5
- decay_rate: float32 [128], replicated, may hold values from 0 to 1, as said below
- skip_gain: float32 [128], replicated, may hold values from 0.5 to 1.5
- bc_prev: bfloat16 [4096, 1024], P('seq'), may hold values from -4 to 4
- dt_prev: float32 [4096, 128], P('seq', 'fsdp'), may hold values from 0.01 to 0.3
- seg_prev: int32 [4], replicated, may hold values from 1 to 2048, 4096 in all
- grad_prev: bfloat16 [4096, 8192], P('seq', 'fsdp'), may hold values from -6 to 6
Outputs:
- out_next: bfloat16 [4096, 8192], P('seq', 'fsdp')
- grad_values: bfloat16 [4096, 8192], P('seq', 'fsdp')
Inputs may be any that keep to these rules, and one draw needn't show every extreme that they name: `seg_next`: lengths of the rollout's 4 segments in order, summing to 4096. `seg_prev`: lengths of the rollout's 4 segments in order, summing to 4096. `decay_rate`: positive.
All inputs are finite; a program needn't handle non-finite values.
Results may differ from a plain program's by a relative error of at most 0.0064.
Values may be sent and summed in bfloat16 or wider, within the bound.
A program may use at most 192 MiB of HBM per device.

v0:
```python
import functools

import jax
import jax.numpy as jnp
from jax import lax
from jax.experimental import pallas as pl
from jax.experimental.pallas import tpu as pltpu
from jax.sharding import PartitionSpec as P

GW = 4
SPAN = 128
LANES = 128
MESH = pl.DeviceIdType.MESH


def widen(a, c, head_dim):
    per = LANES // head_dim
    lane = lax.broadcasted_iota(jnp.int32, (1, LANES), 1)
    res = a[:, c * per:c * per + 1]
    for k in range(1, per):
        res = jnp.where(lane >= k * head_dim, a[:, c * per + k:c * per + k + 1], res)
    return jnp.broadcast_to(res, (a.shape[0], LANES))


def seg_maker(len_ref):
    bound = []
    total = jnp.int32(0)
    for k in range(len_ref.shape[0] - 1):
        total = total + len_ref[k]
        bound.append(total)

    def seg_of(pos):
        s = jnp.zeros_like(pos)
        for b in bound:
            s = s + (b <= pos).astype(jnp.int32)
        return s

    return seg_of


def local_states(back, dims, len_ref, x_ref, q_ref, dt_ref, decay_ref, work, pre, keep):
    nblocks, heads, groups, head_dim = dims
    cum_s, cum_t, dt_t, fout_s = work
    npair = heads * head_dim // LANES
    pair_group = npair // groups
    seg_of = seg_maker(len_ref)
    slab = lax.axis_index("seq") * (nblocks * SPAN)
    dim0 = lax.broadcasted_iota(jnp.int32, (SPAN, SPAN), 0)
    dim1 = lax.broadcasted_iota(jnp.int32, (SPAN, SPAN), 1)
    tril = (dim0 >= dim1).astype(jnp.float32)
    for c in range(npair):
        pre[0, c] = jnp.zeros((LANES, LANES), jnp.float32)
        keep[0, c] = jnp.ones((1, LANES), jnp.float32)
    for step in range(nblocks):
        b = nblocks - 1 - step if back else step
        rows = slice(b * SPAN, (b + 1) * SPAN)
        dt = dt_ref[rows, :]
        cum = jnp.dot(tril, -(dt * decay_ref[...]), precision=lax.Precision.HIGHEST,
                      preferred_element_type=jnp.float32)
        end = cum[SPAN - 1:SPAN, :]
        cum_s[rows, :] = cum
        cum_t[b] = cum.T
        dt_t[b] = dt.T
        seg = seg_of(slab + b * SPAN + lax.broadcasted_iota(jnp.int32, (SPAN, heads), 0))
        edge = slab + b * SPAN + lax.broadcasted_iota(jnp.int32, (1, heads), 0) * 0
        seg_e = seg_of(edge + (SPAN - 1))
        seg_b = jnp.where(edge == 0, 0, seg_of(edge - 1))
        send = jnp.where(seg == seg_e, jnp.exp(end - cum), 0.0) * dt
        read = jnp.where(seg == seg_b, jnp.exp(cum), 0.0)
        carry = jnp.where(seg_e == seg_b, jnp.exp(end), 0.0)
        f_in = read if back else send
        fout_s[rows, :] = send if back else read
        qt = [q_ref[rows, g * LANES:(g + 1) * LANES].T for g in range(groups)]
        for c in range(npair):
            cols = slice(c * LANES, (c + 1) * LANES)
            sent = (x_ref[rows, cols].astype(jnp.float32) * widen(f_in, c, head_dim)).astype(jnp.bfloat16)
            loc = jnp.dot(qt[c // pair_group], sent, preferred_element_type=jnp.float32)
            wide = widen(carry, c, head_dim)
            pre[step + 1, c] = wide * pre[step, c] + loc
            keep[step + 1, c] = wide * keep[step, c]


def in_block(back, dims, len_ref, x_ref, p_ref, q_ref, dt_ref, skip_ref, work, inside, fexp):
    nblocks, heads, groups, head_dim = dims
    cum_s, cum_t, dt_t, fout_s = work
    npair = heads * head_dim // LANES
    per = LANES // head_dim
    pair_group = npair // groups
    seg_of = seg_maker(len_ref)
    slab = lax.axis_index("seq") * (nblocks * SPAN)
    dim0 = lax.broadcasted_iota(jnp.int32, (SPAN, SPAN), 0)
    dim1 = lax.broadcasted_iota(jnp.int32, (SPAN, SPAN), 1)
    lane = lax.broadcasted_iota(jnp.int32, (1, LANES), 1)

    def one(b, _):
        start = pl.multiple_of(b * SPAN, SPAN)
        rows = pl.ds(start, SPAN)
        seg_i = seg_of(slab + start + dim0)
        seg_j = seg_of(slab + start + dim1)
        order = (dim1 >= dim0) if back else (dim1 <= dim0)
        bias = jnp.where((seg_i == seg_j) & order, 0.0, -jnp.inf)
        cum = cum_s[rows, :]
        dt = dt_ref[rows, :]
        f_out = fout_s[rows, :]
        for g in range(groups):
            gl = slice(g * LANES, (g + 1) * LANES)
            score = lax.dot_general(p_ref[rows, gl], q_ref[rows, gl], (((1,), (1,)), ((), ())),
                                    preferred_element_type=jnp.float32)
            for c in range(g * pair_group, (g + 1) * pair_group):
                cols = slice(c * LANES, (c + 1) * LANES)
                x = x_ref[rows, cols]
                mixes, parts = [], []
                for k in range(per):
                    h = c * per + k
                    col = cum[:, h:h + 1]
                    row = cum_t[b, h:h + 1, :]
                    spread = (row - col) if back else (col - row)
                    w = jnp.exp(spread + bias) * score
                    if not back:
                        w = w * dt_t[b, h:h + 1, :]
                    mixes.append(w.astype(jnp.bfloat16))
                    mine = (lane >= k * head_dim) & (lane < (k + 1) * head_dim)
                    parts.append(jnp.where(mine, x, jnp.zeros_like(x)))
                acc = jnp.dot(jnp.concatenate(mixes, 1), jnp.concatenate(parts, 0),
                              preferred_element_type=jnp.float32)
                if back:
                    acc = acc * widen(dt, c, head_dim)
                inside[c, rows, :] = acc + widen(skip_ref[...], c, head_dim) * x.astype(jnp.float32)
                fexp[c, rows, :] = widen(f_out, c, head_dim)
        return 0

    lax.fori_loop(0, nblocks, one, 0)


HOP_CHUNKS = 5


def chain_kernel(count, dims, len_ref, x_ref, p_ref, q_ref, dt_ref, decay_ref, skip_ref,
                 lenb_ref, xb_ref, pb_ref, qb_ref, dtb_ref,
                 out_ref, grad_ref, *scratch):
    work, work_b, rest = scratch[:4], scratch[4:8], scratch[12:]
    inside_b, fexp_b, pre_b, keep_b = scratch[8:12]
    inside, fexp, pre, keep, inbox, outbox, in_b, out_b, s_sem, r_sem, sb_sem, rb_sem = rest
    nblocks, heads, groups, head_dim = dims
    npair = heads * head_dim // LANES
    pair_group = npair // groups
    me = lax.axis_index("seq")
    low, high = me == 0, me == count - 1

    barrier = pltpu.get_barrier_semaphore()

    @pl.when(jnp.logical_not(low))
    def _():
        pl.semaphore_signal(barrier, inc=1, device_id={"seq": me - 1}, device_id_type=MESH)

    @pl.when(jnp.logical_not(high))
    def _():
        pl.semaphore_signal(barrier, inc=1, device_id={"seq": me + 1}, device_id_type=MESH)

    local_states(False, dims, len_ref, x_ref, q_ref, dt_ref, decay_ref, work, pre, keep)
    local_states(True, dims, lenb_ref, xb_ref, qb_ref, dtb_ref, decay_ref, work_b, pre_b, keep_b)

    @pl.when(low)
    def _():
        inbox[...] = jnp.zeros_like(inbox)

    @pl.when(high)
    def _():
        in_b[...] = jnp.zeros_like(in_b)

    pl.semaphore_wait(barrier, jnp.where(low, 0, 1) + jnp.where(high, 0, 1))

    def hop(back, c):
        return pltpu.make_async_remote_copy(
            src_ref=(out_b if back else outbox).at[c], dst_ref=(in_b if back else inbox).at[c],
            send_sem=(sb_sem if back else s_sem).at[c], recv_sem=(rb_sem if back else r_sem).at[c],
            device_id={"seq": me - 1 if back else me + 1}, device_id_type=MESH)

    def relay(back, c):
        first, last = (high, low) if back else (low, high)
        kp, pr = (keep_b, pre_b) if back else (keep, pre)

        @pl.when(jnp.logical_not(first))
        def _():
            hop(back, c).wait_recv()

        @pl.when(jnp.logical_not(last))
        def _():
            state = (in_b if back else inbox)[c].astype(jnp.float32)
            (out_b if back else outbox)[c] = (kp[nblocks, c] * state + pr[nblocks, c]).astype(jnp.bfloat16)
            hop(back, c).start()

    def finish(back, c):
        kp, pr, ins, fx, vec, out = (
            (keep_b, pre_b, inside_b, fexp_b, pb_ref, grad_ref) if back
            else (keep, pre, inside, fexp, p_ref, out_ref))
        g = c // pair_group
        cols = pl.ds(pl.multiple_of(c * LANES, LANES), LANES)
        gl = pl.ds(pl.multiple_of(g * LANES, LANES), LANES)
        state = (in_b if back else inbox)[c].astype(jnp.float32)
        for step in range(nblocks):
            b = nblocks - 1 - step if back else step
            rows = slice(b * SPAN, (b + 1) * SPAN)
            entering = (kp[step, c] * state + pr[step, c]).astype(jnp.bfloat16)
            y = jnp.dot(vec[rows, gl], entering, preferred_element_type=jnp.float32)
            out[rows, cols] = (ins[c, rows, :] + fx[c, rows, :] * y).astype(jnp.bfloat16)

    lag = (2 * me - (count - 1)) * HOP_CHUNKS
    up_first = lag < 0
    gap = jnp.where(up_first, -lag, lag)
    block_at = jnp.where(gap >= npair, npair, 0)

    def step_of(i, _):
        @pl.when(i == block_at)
        def _():
            in_block(False, dims, len_ref, x_ref, p_ref, q_ref, dt_ref, skip_ref, work, inside, fexp)
            in_block(True, dims, lenb_ref, xb_ref, pb_ref, qb_ref, dtb_ref, skip_ref, work_b, inside_b, fexp_b)

        for back in (False, True):
            leads = jnp.logical_not(up_first) if back else up_first
            c = i - jnp.where(leads, 0, gap)

            @pl.when((c >= 0) & (c < npair))
            def _(back=back, c=c):
                relay(back, c)

            done = jnp.where(leads, i - npair, c)

            @pl.when((done >= 0) & (done < npair))
            def _(back=back, done=done):
                finish(back, done)

        return 0

    lax.fori_loop(0, npair + jnp.maximum(gap, npair), step_of, 0)

    def drain(c, _):
        @pl.when(jnp.logical_not(high))
        def _():
            hop(False, c).wait_send()

        @pl.when(jnp.logical_not(low))
        def _():
            hop(True, c).wait_send()

        return 0

    lax.fori_loop(0, npair, drain, 0)


def sizes_of(x, p_vec, dt):
    tokens, width = x.shape
    heads = dt.shape[1]
    dims = (tokens // SPAN, heads, p_vec.shape[1] // LANES, width // heads)
    nblocks, npair = dims[0], width // LANES
    f32 = jnp.float32
    work = [pltpu.VMEM((tokens, heads), f32), pltpu.VMEM((nblocks, heads, SPAN), f32),
            pltpu.VMEM((nblocks, heads, SPAN), f32), pltpu.VMEM((tokens, heads), f32)]
    kept = [(npair, tokens, LANES), (npair, tokens, LANES),
            (nblocks + 1, npair, LANES, LANES), (nblocks + 1, npair, 1, LANES)]
    return dims, npair, work, kept


VM = pl.BlockSpec(memory_space=pltpu.VMEM)
SM = pl.BlockSpec(memory_space=pltpu.SMEM)


def chains(lengths, x, p_vec, q_vec, dt, decay, skip, *back):
    dims, npair, work, kept = sizes_of(x, p_vec, dt)
    box = pltpu.VMEM((npair, LANES, LANES), jnp.bfloat16)
    sem = pltpu.SemaphoreType.DMA((npair,))
    return pl.pallas_call(
        functools.partial(chain_kernel, lax.axis_size("seq"), dims),
        out_shape=[jax.ShapeDtypeStruct(x.shape, jnp.bfloat16)] * 2,
        in_specs=[SM] + [VM] * 6 + [SM] + [VM] * 4,
        out_specs=[VM] * 2,
        scratch_shapes=(work * 2 + [pltpu.VMEM(k, jnp.float32) for k in kept] * 2
                        + [box] * 4 + [sem] * 4),
        compiler_params=pltpu.CompilerParams(
            collective_id=0, has_side_effects=True, vmem_limit_bytes=56 * 1024 * 1024),
        cost_estimate=pl.CostEstimate(flops=40_000_000_000, bytes_accessed=40_000_000, transcendentals=0),
        name="chains",
    )(lengths, x, p_vec, q_vec, dt, decay, skip, *back)


PIECES = 4


def gather_kernel(count, h_ref, w_ref, bc_ref, dt_ref,
                  held, acc, bc_out, bc_in, dt_out, dt_in,
                  ring_s, ring_r, side_s, side_r, x_s, x_r):
    me, f = lax.axis_index("seq"), lax.axis_index("fsdp")
    n = count // 2
    half_ring = n // 2
    core, chip = me % 2, me // 2
    r = jnp.where(chip % 2 == 0, chip // 2, n - 1 - chip // 2)
    rows = w_ref.shape[0]
    piece = rows // PIECES
    wide = bc_ref.shape[1]

    def id_of(pos, which):
        p = (pos + 2 * n) % n
        up = p < half_ring
        return jnp.where(up, p * 2, (n - 1 - p) * 2 + 1) * 2 + which

    nxt, prv, partner = id_of(r + 1, core), id_of(r - 1, core), chip * 2 + 1 - core

    barrier = pltpu.get_barrier_semaphore()
    for peer in (nxt, prv, partner):
        pl.semaphore_signal(barrier, inc=1, device_id={"seq": peer}, device_id_type=MESH)
    pl.semaphore_signal(barrier, inc=1, device_id={"fsdp": 1 - f}, device_id_type=MESH)
    pl.semaphore_wait(barrier, 4)

    def part(p):
        return pl.ds(p * piece, piece)

    def origin(step, p, which):
        return id_of(r - step if p < PIECES // 2 else r + step, which)

    def ring_copy(step, p, src):
        return pltpu.make_async_remote_copy(
            src_ref=src, dst_ref=held.at[origin(step, p, core), part(p), :],
            send_sem=ring_s.at[step, p], recv_sem=ring_r.at[step, p],
            device_id={"seq": nxt if p < PIECES // 2 else prv}, device_id_type=MESH)

    def side_copy(step, p, src):
        return pltpu.make_async_remote_copy(
            src_ref=src, dst_ref=held.at[origin(step, p, core), part(p), :],
            send_sem=side_s.at[step, p], recv_sem=side_r.at[step, p],
            device_id={"seq": partner}, device_id_type=MESH)

    def landed(step, p):
        return held.at[origin(step, p, core), part(p), :]

    for p in range(PIECES):
        ring_copy(0, p, w_ref.at[part(p), :]).start()
    for p in range(PIECES):
        side_copy(0, p, w_ref.at[part(p), :]).start()

    def columns(seq_index, first):
        start = (seq_index * 2 + f) * rows + first
        return h_ref[:, pl.ds(pl.multiple_of(start, rows // 2), rows // 2)]

    def mac(step, which):
        half = rows // 2
        lo, hi = origin(step, 0, which), origin(step, PIECES - 1, which)
        left = jnp.concatenate([columns(lo, 0), columns(hi, half)], axis=1)
        right = jnp.concatenate([held[lo, 0:half, :], held[hi, half:, :]], axis=0)
        acc[...] += jnp.dot(left, right, preferred_element_type=jnp.float32)

    acc[...] = jnp.dot(jnp.concatenate([columns(me, 0), columns(me, rows // 2)], axis=1), w_ref[...],
                       preferred_element_type=jnp.float32)

    def one(step, _):
        for p in (0, PIECES // 2, 1, PIECES // 2 + 1):
            ring_copy(step, p, landed(step, p)).wait_recv()

            @pl.when(step < n - 2)
            def _(p=p):
                ring_copy(step + 1, p, landed(step + 1, p)).start()

            side_copy(step + 1, p, landed(step + 1, p)).start()
        mac(step + 1, core)
        for p in range(PIECES):
            side_copy(step, p, landed(step, p)).wait_recv()
        mac(step, 1 - core)
        return 0

    lax.fori_loop(0, n - 1, one, 0)
    for p in range(PIECES):
        side_copy(n - 1, p, landed(n - 1, p)).wait_recv()
    mac(n - 1, 1 - core)

    def cross(src, dst, k):
        return pltpu.make_async_remote_copy(
            src_ref=src, dst_ref=dst, send_sem=x_s.at[k], recv_sem=x_r.at[k],
            device_id={"fsdp": 1 - f}, device_id_type=MESH)

    def side_of(which):
        return pl.ds(pl.multiple_of(which * wide, wide), wide)

    bc_out[...] = acc[:, side_of(1 - f)]
    dt_out[...] = acc[:, 2 * wide:]
    cross(bc_out, bc_in, 0).start()
    cross(dt_out, dt_in, 1).start()

    def drain(step, _):
        for p in range(PIECES):
            @pl.when(step < n - 1)
            def _(p=p):
                ring_copy(step, p, landed(step, p)).wait_send()

            side_copy(step, p, landed(step, p)).wait_send()
        return 0

    lax.fori_loop(0, n, drain, 0)
    cross(bc_out, bc_in, 0).wait()
    bc_ref[...] = (acc[:, side_of(f)] + bc_in[...]).astype(jnp.bfloat16)
    cross(dt_out, dt_in, 1).wait()
    dt_ref[...] = acc[:, 2 * wide:] + dt_in[...]


def gathered_sums(hidden, shard, wide):
    count = lax.axis_size("seq")
    tokens, total = hidden.shape[0], shard.shape[1]
    f32, bf16 = jnp.float32, jnp.bfloat16
    n = count // 2
    dma = pltpu.SemaphoreType.DMA
    return pl.pallas_call(
        functools.partial(gather_kernel, count),
        out_shape=[jax.ShapeDtypeStruct((tokens, wide), bf16),
                   jax.ShapeDtypeStruct((tokens, total - 2 * wide), f32)],
        in_specs=[VM] * 2,
        out_specs=[VM] * 2,
        scratch_shapes=[
            pltpu.VMEM((count,) + shard.shape, bf16),
            pltpu.VMEM((tokens, total), f32),
            pltpu.VMEM((tokens, wide), f32), pltpu.VMEM((tokens, wide), f32),
            pltpu.VMEM((tokens, total - 2 * wide), f32), pltpu.VMEM((tokens, total - 2 * wide), f32),
            dma((n, PIECES)), dma((n, PIECES)), dma((n, PIECES)), dma((n, PIECES)), dma((2,)), dma((2,)),
        ],
        compiler_params=pltpu.CompilerParams(
            collective_id=1, has_side_effects=True, vmem_limit_bytes=32 * 1024 * 1024),
        cost_estimate=pl.CostEstimate(flops=40_000_000_000, bytes_accessed=40_000_000, transcendentals=0),
        name="gather_project",
    )(hidden, shard)


def body(
    hidden_next, values_next, seg_next, proj_bc, proj_dt, dt_bias, decay_rate, skip_gain,
    bc_prev, dt_prev, seg_prev, grad_prev,
):
    tokens_dev = hidden_next.shape[0]
    bc_width = proj_bc.shape[1]
    heads_all = proj_dt.shape[1]
    fsdp_count = lax.axis_size("fsdp")
    fsdp_place = lax.axis_index("fsdp")
    seq_count = lax.axis_size("seq")
    heads_dev = heads_all // fsdp_count
    state_dim = bc_width // (2 * GW)
    per_group = heads_all // GW
    groups_dev = max(1, heads_dev // per_group)
    first_head = fsdp_place * heads_dev
    first_group = first_head // per_group
    rows_dev = proj_bc.shape[0]
    half = bc_width // 2
    gw = groups_dev * state_dim

    blocks = []
    for f in range(fsdp_count):
        g0 = (f * heads_dev // per_group) * state_dim
        blocks.append([proj_bc[:, g0:g0 + gw], proj_bc[:, half + g0:half + g0 + gw]])
    ring = fsdp_count == 2 and seq_count % 4 == 0 and rows_dev % (2 * LANES) == 0 and heads_all == LANES
    if ring:
        shard = jnp.concatenate([*blocks[0], *blocks[1], proj_dt], axis=1)
        bc_next, dt_sum = gathered_sums(hidden_next, shard, 2 * gw)
        dt_sum = lax.dynamic_slice_in_dim(dt_sum, first_head, heads_dev, 1)
    else:
        pieces = []
        for f in range(fsdp_count):
            pieces += [*blocks[f], proj_dt[:, f * heads_dev:(f + 1) * heads_dev]]
        weights = lax.all_gather(jnp.concatenate(pieces, axis=1), "seq", axis=0, tiled=True)
        owned = lax.dynamic_slice_in_dim(
            hidden_next.reshape(tokens_dev, seq_count, fsdp_count, rows_dev), fsdp_place, 1, 2
        ).reshape(tokens_dev, seq_count * rows_dev)
        sums = lax.psum_scatter(jnp.dot(owned, weights, preferred_element_type=jnp.float32),
                                "fsdp", scatter_dimension=1, tiled=True)
        bc_next, dt_sum = sums[:, :2 * gw].astype(jnp.bfloat16), sums[:, 2 * gw:]

    decay = lax.dynamic_slice_in_dim(decay_rate, first_head, heads_dev, 0)[None]
    skip = lax.dynamic_slice_in_dim(skip_gain, first_head, heads_dev, 0)[None]
    bias = lax.dynamic_slice_in_dim(dt_bias, first_head, heads_dev, 0)[None]

    b_prev = lax.dynamic_slice_in_dim(bc_prev, first_group * state_dim, gw, 1)
    c_prev = lax.dynamic_slice_in_dim(bc_prev, half + first_group * state_dim, gw, 1)
    b_next, c_next = bc_next[:, :gw], bc_next[:, gw:]
    dt_next = jax.nn.softplus(dt_sum + bias)
    out_next, grad_values = chains(
        seg_next, values_next, c_next, b_next, dt_next, decay, skip,
        seg_prev, grad_prev, b_prev, c_prev, dt_prev)
    return (out_next, grad_values)


def solution(mesh):
    in_specs = (
        P("seq", None), P("seq", "fsdp"), P(), P(("seq", "fsdp"), None), P(("seq", "fsdp"), None),
        P(), P(), P(), P("seq", None), P("seq", "fsdp"), P(), P("seq", "fsdp"),
    )
    out_specs = (P("seq", "fsdp"), P("seq", "fsdp"))
    return jax.shard_map(body, mesh=mesh, in_specs=in_specs, out_specs=out_specs, check_vma=False)
```

profile of v0, /device:TPU:0, one launch (start us, length us, event | category | flops | bytes accessed | tf_op | source)
XLA Modules:
  0.0 153.6 jit_solution(7069709090662371676)
XLA Ops:
  0.7 0.7 dynamic_slice.19
  1.4 1.3 dynamic-slice_bitcast_fusion
  2.7 1.6 %copy.14.dtb_ref = f32[256,64]{1,0:T(8,128)} copy(f32[256,64]{0,1:T(8,128)} %param.21) | data formatting | bytes 131072 | tf_op args[9]
  4.3 0.9 slice_dynamic-update-slice_fusion.3
  5.2 0.9 slice_dynamic-update-slice_fusion.2
  6.2 0.9 slice_dynamic-update-slice_fusion.1
  7.1 0.9 slice_dynamic-update-slice_fusion
  8.0 0.9 constant_dynamic-update-slice_fusion.w_ref
  8.9 0.0 copy-start
  8.9 2.2 %copy-done = bf16[256,8192]{1,0:T(8,128)(2,1)S(1)} copy-done((bf16[256,8192]{1,0:T(8,128)(2,1)S(1)}, bf16[256,8192]{1,0:T(8,128)(2,1)}, u32[]{:S(2)}) %copy-start) | copy-done | bytes 4194328
  11.0 0.0 copy-start.2
  11.0 68.7 %gather_project.1 = (bf16[256,512]{1,0:T(8,128)(2,1)S(1)}, f32[256,128]{1,0:T(8,128)S(1)}) custom-call(bf16[256,8192]{1,0:T(8,128)(2,1)S(1)} %copy-done, bf16[256,1152]{1,0:T(8,128)(2,1)S(1)} %constant_dynamic-update-slice_fusion.w_ref), custom_call_target="tpu_custom_call" | custom-call | flops 40000000000 | bytes 40000000 | tf_op jit(solution)/shard_map/gather_project/pallas_call | solution.py:409
  79.8 0.8 compare_select_fusion.dt_ref
  80.6 0.0 copy-done.2
  80.6 0.8 constant_dynamic-slice_fusion
  81.4 67.6 %chains.1 = (bf16[256,4096]{1,0:T(8,128)(2,1)}, bf16[256,4096]{1,0:T(8,128)(2,1)}) custom-call(s32[4]{0:T(128)} %len_ref.1, bf16[256,4096]{1,0:T(8,128)(2,1)} %x_ref.1, bf16[256,256]{1,0:T(8,128)(2,1)} %get-tuple-element.12.p_ref, bf16[256,256]{1,0:T(8,128)(2,1)} %get-tuple-element.13.q_ref, f32[256,64]{1,0:T(8,128)} %compare_select_fusion.dt_ref, ...), custom_call_target="tpu_custom_call" | custom-call | flops 40000000000 | bytes 40000000 | tf_op jit(solution)/shard_map/chains/pallas_call | solution.py:272
  149.0 0.0 copy-start.1
  149.0 3.3 %copy.21 = bf16[256,4096]{1,0:T(8,128)(2,1)} copy(bf16[256,4096]{1,0:T(8,128)(2,1)} %get-tuple-element.16) | data formatting | bytes 4194304
  152.3 0.0 copy-done.1
  152.3 1.3 copy.22
Async XLA Ops:
  8.9 2.2 %copy-start = (bf16[256,8192]{1,0:T(8,128)(2,1)S(1)}, bf16[256,8192]{1,0:T(8,128)(2,1)}, u32[]{:S(2)}) copy-start(bf16[256,8192]{1,0:T(8,128)(2,1)} %h_ref.1) | copy-start | bytes 12582916
  11.0 69.6 %copy-start.2 = (bf16[256,1024]{1,0:T(8,128)(2,1)S(1)}, bf16[256,1024]{1,0:T(8,128)(2,1)}, u32[]{:S(2)}) copy-start(bf16[256,1024]{1,0:T(8,128)(2,1)} %param.20) | copy-start | bytes 1572868
  149.0 3.3 %copy-start.1 = (bf16[256,4096]{1,0:T(8,128)(2,1)S(1)}, bf16[256,4096]{1,0:T(8,128)(2,1)}, u32[]{:S(2)}) copy-start(bf16[256,4096]{1,0:T(8,128)(2,1)} %get-tuple-element.17) | copy-start | bytes 6291460
where the time goes:
time: 154 us
  Pallas kernels  136 us (88%)
  local copies, waits for them, and re-layouts  15.8 us (10%)
    pallas_call x1, Pallas kernels, gathered_sums(): pl.pallas_call(functools.partial(gather_kernel, count), out_shape=[jax.Sh...  68.7 us
    pallas_call x1, Pallas kernels, chains(): pl.pallas_call(functools.partial(chain_kernel, lax.axis_size('seq'), dims...  67.6 us
    unnamed x13, local copies, waits for them, and re-layouts  12 us

commit v1 on v0

--- a/solution.py
+++ b/solution.py
@@ -80,7 +80,7 @@
             keep[step + 1, c] = wide * keep[step, c]
 
 
-def in_block(back, dims, len_ref, x_ref, p_ref, q_ref, dt_ref, skip_ref, work, inside, fexp):
+def in_block(back, dims, len_ref, x_ref, p_ref, q_ref, dt_ref, skip_ref, work, inside, fexp, span=None):
     nblocks, heads, groups, head_dim = dims
     cum_s, cum_t, dt_t, fout_s = work
     npair = heads * head_dim // LANES
@@ -129,7 +129,8 @@
                 fexp[c, rows, :] = widen(f_out, c, head_dim)
         return 0
 
-    lax.fori_loop(0, nblocks, one, 0)
+    first, last = (0, nblocks) if span is None else span
+    lax.fori_loop(first, last, one, 0)
 
 
 HOP_CHUNKS = 5
@@ -426,6 +427,423 @@
     )(hidden, shard)
 
 
+Z_LAG = 4
+CORE_LAG = 3
+
+
+def fused_kernel(count, dims, len_ref, lenb_ref, bias_in, decay_in, skip_in, pdt_ref, dtt_ref,
+                 h_hbm, x_hbm, w_hbm, bcp_hbm, g_hbm, out_hbm, grad_hbm,
+                 hid, held, yout, xv, gv, bp, cp, bn, cn, acc, dtn, dtp, decay_ref, skip_ref,
+                 *scratch):
+    work, work_b = scratch[:4], scratch[4:8]
+    kept = (scratch[8:12], scratch[12:16])
+    lout, lin, xout, xin, zout, zin, eout, ein, kv, ksib, kxo, kxi = (
+        (scratch[16 + 2 * i], scratch[17 + 2 * i]) for i in range(12))
+    (ld, ring_s, ring_r, side_s, side_r, y_s, y_r, l_s, l_r, k_s, k_r, c_s, c_r, z_s, z_r,
+     e_s, e_r, o_sem) = scratch[40:]
+    nblocks, heads, groups, head_dim = dims
+    npair = heads * head_dim // LANES
+    pair_group = npair // groups
+    half_pairs = npair // 2
+    me, f = lax.axis_index("seq"), lax.axis_index("fsdp")
+    core, chip = me % 2, me // 2
+    xpos, zpos, nz = chip % 2, chip // 2, count // 4
+    n = count // 2
+    half_ring = n // 2
+    full = half_ring - 1
+    far = 2 * full + 1
+    gw = groups * LANES
+    wrows = w_hbm.shape[0]
+    prow = held.shape[2] // 2
+    r = jnp.where(xpos == 0, zpos, n - 1 - zpos)
+
+    def chip_at(pos):
+        p = (pos + 2 * n) % n
+        return jnp.where(p < half_ring, p * 2, (n - 1 - p) * 2 + 1)
+
+    nxt, prv = chip_at(r + 1) * 2 + core, chip_at(r - 1) * 2 + core
+    partner = chip * 2 + 1 - core
+    xpeer = (zpos * 2 + 1 - xpos) * 2 + core
+    own, other = core * 2 + f, core * 2 + 1 - f
+
+    def at_cols(start):
+        return pl.ds(pl.multiple_of(start, LANES), gw)
+
+    def load(src, dst, k):
+        return pltpu.make_async_copy(src, dst, ld.at[k])
+
+    w_half = w_hbm.shape[1] // 2
+    w_loads = [
+        load(w_hbm.at[:, at_cols(f * gw)], held.at[chip, own, 0:wrows, 0:gw], 0),
+        load(w_hbm.at[:, at_cols(w_half + f * gw)], held.at[chip, own, 0:wrows, gw:2 * gw], 1),
+        load(w_hbm.at[:, at_cols((1 - f) * gw)], yout.at[0:wrows, 0:gw], 2),
+        load(w_hbm.at[:, at_cols(w_half + (1 - f) * gw)], yout.at[0:wrows, gw:2 * gw], 3),
+    ]
+    b_loads = [
+        load(g_hbm, gv, 4),
+        load(bcp_hbm.at[:, at_cols(f * gw)], bp, 5),
+        load(bcp_hbm.at[:, at_cols(w_half + f * gw)], cp, 6),
+    ]
+    h_load, x_load = load(h_hbm, hid, 7), load(x_hbm, xv, 8)
+    for copy in (*w_loads, *b_loads, h_load, x_load):
+        copy.start()
+
+    barrier = pltpu.get_barrier_semaphore()
+    for peer in (partner, xpeer):
+        pl.semaphore_signal(barrier, inc=1, device_id={"seq": peer}, device_id_type=MESH)
+    pl.semaphore_signal(barrier, inc=1, device_id={"fsdp": 1 - f}, device_id_type=MESH)
+
+    @pl.when(zpos > 0)
+    def _():
+        pl.semaphore_signal(barrier, inc=1, device_id={"seq": me - 4}, device_id_type=MESH)
+
+    @pl.when(zpos < nz - 1)
+    def _():
+        pl.semaphore_signal(barrier, inc=1, device_id={"seq": me + 4}, device_id_type=MESH)
+
+    lane = lax.broadcasted_iota(jnp.int32, (LANES, LANES), 1)
+    top = pdt_ref[0:LANES, :].astype(jnp.float32)
+    low = pdt_ref[LANES:2 * LANES, :].astype(jnp.float32)
+    pack0 = jnp.where(lane < heads, top, pltpu.roll(low, heads, 1))
+    pack1 = jnp.where(lane < heads, pltpu.roll(top, heads, 1), low)
+    mine = jnp.where(f == 0, pack0, pack1).astype(jnp.bfloat16)
+    theirs = jnp.where(f == 0, pack1, pack0).astype(jnp.bfloat16)
+    strips = 2 * gw // LANES
+    strip = LANES // strips
+    for k in range(strips):
+        lanes = slice(k * LANES, (k + 1) * LANES)
+        held[chip, own, wrows:wrows + strip, lanes] = mine[k * strip:(k + 1) * strip, :]
+        yout[wrows:wrows + strip, lanes] = theirs[k * strip:(k + 1) * strip, :]
+    decay_ref[...] = jnp.where(f == 0, decay_in[:, 0:heads], decay_in[:, heads:2 * heads])
+    skip_ref[...] = jnp.where(f == 0, skip_in[:, 0:heads], skip_in[:, heads:2 * heads])
+    bias = jnp.where(f == 0, bias_in[:, 0:heads], bias_in[:, heads:2 * heads])
+    for b in range(nblocks):
+        dtp[b * SPAN:(b + 1) * SPAN, :] = dtt_ref[:, b * SPAN:(b + 1) * SPAN].T
+
+    pl.semaphore_wait(barrier, 3 + jnp.where(zpos > 0, 1, 0) + jnp.where(zpos < nz - 1, 1, 0))
+    for copy in w_loads:
+        copy.wait()
+
+    def rows_of(j):
+        return pl.ds((j % 2) * prow, prow)
+
+    def piece(where, j, mine=True):
+        base = (core if mine else 1 - core) * 2
+        return held.at[where, base + (f if j < 2 else 1 - f), rows_of(j), :]
+
+    def remote(src, dst, s, rv, **peer):
+        return pltpu.make_async_remote_copy(src_ref=src, dst_ref=dst, send_sem=s, recv_sem=rv,
+                                            device_id=peer, device_id_type=MESH)
+
+    def ring(d, k, j, arrived=False):
+        away = k if arrived else k - 1
+        ref = piece(chip_at(r - away if d == 0 else r + away), j)
+        return remote(ref, ref, ring_s.at[d, k - 1, j], ring_r.at[d, k - 1, j],
+                      seq=nxt if d == 0 else prv)
+
+    def chip_of(u):
+        return chip_at(r - u if u <= full else (r + (u - full) if u < far else r + half_ring))
+
+    def side(u, j, arrived=False):
+        ref = piece(chip_of(u), j, not arrived)
+        return remote(ref, ref, side_s.at[u, j], side_r.at[u, j], seq=partner)
+
+    def cross(j, arrived=False):
+        dst = held.at[chip, other, rows_of(j), :]
+        dst = dst if arrived else held.at[chip, own, rows_of(j), :]
+        return remote(yout.at[rows_of(j), :], dst, y_s.at[j], y_r.at[j], fsdp=1 - f)
+
+    def begin(j):
+        ring(0, 1, j).start()
+        ring(1, 1, j).start()
+        side(0, j).start()
+
+    for j in range(2):
+        cross(j).start()
+        begin(j)
+
+    def receive(k, j):
+        for d in range(2):
+            if k > full and (j < 2) != (d == 0):
+                continue
+            ring(d, k, j, True).wait_recv()
+            if k < full or (k == full and (j < 2) == (d == 0)):
+                ring(d, k + 1, j).start()
+            side(far if k > full else (k if d == 0 else full + k), j).start()
+
+    def mac(u, first=False):
+        for j in range(4):
+            side(u, j, True).wait_recv()
+        q = chip_of(u)
+        wide = 4 * wrows
+        left = hid[:, pl.ds(pl.multiple_of(q * wide, wide), wide)]
+        main = jnp.dot(left, jnp.concatenate([held[q, s, 0:wrows, :] for s in range(4)], axis=0),
+                       preferred_element_type=jnp.float32)
+        packs = jnp.concatenate(
+            [held[q, s, wrows:wrows + strip, k * LANES:(k + 1) * LANES]
+             for s in range(4) for k in range(strips)], axis=0)
+        parts = [jnp.dot(jnp.concatenate([left[:, s * wrows + o:s * wrows + o + LANES] for s in range(4)], axis=1),
+                         packs, preferred_element_type=jnp.float32) for o in (0, LANES)]
+        for at, value in ((0, main), (2 * gw, parts[0]), (2 * gw + LANES, parts[1])):
+            cols = slice(at, at + value.shape[1])
+            acc[:, cols] = value if first else acc[:, cols] + value
+
+    def my_half(back):
+        return core * half_pairs
+
+    def exchange(back):
+        pre, keep = kept[back][2:]
+        for c in range(npair):
+            kv[back][c:c + 1, :] = keep[nblocks, c]
+        remote(kv[back], ksib[back], k_s.at[back], k_r.at[back], seq=partner).start()
+
+        def put(i, _):
+            lout[back][i] = pre[nblocks, (1 - core) * half_pairs + i].astype(jnp.bfloat16)
+            remote(lout[back].at[i], lin[back].at[i], l_s.at[back, i], l_r.at[back, i], seq=partner).start()
+            return 0
+
+        lax.fori_loop(0, half_pairs, put, 0)
+
+    def lead_core(back):
+        return (core == 1) if back else (core == 0)
+
+    def lead_x(back):
+        return (xpos == 1) if back else (xpos == 0)
+
+    def row(ref, i):
+        return ref[pl.ds(i, 1), :]
+
+    def x_copy(back, i):
+        return remote(xout[back].at[i], xin[back].at[i], c_s.at[back, i], c_r.at[back, i], seq=xpeer)
+
+    def kx_copy(back):
+        return remote(kxo[back], kxi[back], k_s.at[2 + back], k_r.at[2 + back], seq=xpeer)
+
+    def combine(back):
+        pre = kept[back][2]
+        rows = pl.ds(pl.multiple_of(core * half_pairs, half_pairs), half_pairs)
+        remote(kv[back], ksib[back], k_s.at[back], k_r.at[back], seq=partner).wait_recv()
+        kxo[back][...] = kv[back][rows, :] * ksib[back][rows, :]
+        kx_copy(back).start()
+
+        def put(i, _):
+            g = core * half_pairs + i
+            remote(lout[back].at[i], lin[back].at[i], l_s.at[back, i], l_r.at[back, i], seq=partner).wait_recv()
+            lead = lead_core(back)
+            total = (pre[nblocks, g] * jnp.where(lead, row(ksib[back], g), 1.0)
+                     + lin[back][i].astype(jnp.float32) * jnp.where(lead, 1.0, row(kv[back], g)))
+            xout[back][i] = total.astype(jnp.bfloat16)
+            x_copy(back, i).start()
+            return 0
+
+        lax.fori_loop(0, half_pairs, put, 0)
+
+    def z_copy(back, i):
+        return remote(zout[back].at[i], zin[back].at[i], z_s.at[back, i], z_r.at[back, i],
+                      seq=me - 4 if back else me + 4)
+
+    def e_copy(back, i):
+        return remote(eout[back].at[i], ein[back].at[i], e_s.at[back, i], e_r.at[back, i], seq=partner)
+
+    def out_copy(back, c):
+        cols = pl.ds(pl.multiple_of(c * LANES, LANES), LANES)
+        src, dst = (gv, grad_hbm) if back else (xv, out_hbm)
+        return pltpu.make_async_copy(src.at[:, cols], dst.at[:, cols], o_sem.at[back, c])
+
+    def finish(back, c, state):
+        ins, fx, pre, keep = kept[back]
+        vec, out = (bp, gv) if back else (cn, xv)
+        cols = pl.ds(pl.multiple_of(c * LANES, LANES), LANES)
+        gl = pl.ds(pl.multiple_of((c // pair_group) * LANES, LANES), LANES)
+        for step in range(nblocks):
+            b = nblocks - 1 - step if back else step
+            rows = slice(b * SPAN, (b + 1) * SPAN)
+            entering = state if step == 0 else keep[step, c] * state + pre[step, c]
+            y = jnp.dot(vec[rows, gl], entering.astype(jnp.bfloat16), preferred_element_type=jnp.float32)
+            out[rows, cols] = (ins[c, rows, :] + fx[c, rows, :] * y).astype(jnp.bfloat16)
+        out_copy(back, c).start()
+
+    def relay(back, i):
+        pre = kept[back][2]
+        g = core * half_pairs + i
+        z_first, z_last = (zpos == nz - 1, zpos == 0) if back else (zpos == 0, zpos == nz - 1)
+        x_copy(back, i).wait_recv()
+
+        @pl.when(jnp.logical_not(z_first))
+        def _():
+            z_copy(back, i).wait_recv()
+
+        k_own, k_peer = row(kxo[back], i), row(kxi[back], i)
+        l_own, l_peer = xout[back][i].astype(jnp.float32), xin[back][i].astype(jnp.float32)
+        state = jnp.where(z_first, 0.0, zin[back][i].astype(jnp.float32))
+        lead = lead_x(back)
+        zout[back][i] = (k_own * k_peer * state + l_own * jnp.where(lead, k_peer, 1.0)
+                         + l_peer * jnp.where(lead, 1.0, k_own)).astype(jnp.bfloat16)
+
+        @pl.when(jnp.logical_not(z_last))
+        def _():
+            z_copy(back, i).start()
+
+        state = jnp.where(lead, state, k_peer * state + l_peer)
+        head = lead_core(back)
+        k_lead = jnp.where(head, row(kv[back], g), row(ksib[back], g))
+        l_lead = jnp.where(head, pre[nblocks, g], lin[back][i].astype(jnp.float32))
+        after = k_lead * state + l_lead
+        eout[back][i] = jnp.where(head, after, state).astype(jnp.bfloat16)
+        e_copy(back, i).start()
+        finish(back, g, jnp.where(head, state, after))
+
+    def settle(back, i):
+        e_copy(back, i).wait_recv()
+        finish(back, (1 - core) * half_pairs + i, ein[back][i].astype(jnp.float32))
+
+    for copy in b_loads:
+        copy.wait()
+    local_states(True, dims, lenb_ref, gv, cp, dtp, decay_ref, work_b, *kept[1][2:])
+    for j in range(2):
+        cross(j, True).wait_recv()
+        begin(j + 2)
+    exchange(1)
+    receive(1, 0)
+    receive(1, 1)
+
+    def block(back, b):
+        if back:
+            in_block(True, dims, lenb_ref, gv, bp, cp, dtp, skip_ref, work_b, *kept[1][:2], span=(b, b + 1))
+        else:
+            in_block(False, dims, len_ref, xv, cn, bn, dtn, skip_ref, work, *kept[0][:2])
+
+    block(True, 0)
+    receive(1, 2)
+    receive(1, 3)
+    block(True, 1)
+    h_load.wait()
+    for k in range(2, full + 1):
+        for j in range(4):
+            receive(k, j)
+            if j == 1 and k == full:
+                combine(1)
+        if k == 2:
+            mac(0, True)
+        for u in (k - 1, full + k - 1):
+            mac(u)
+    for u in (full, 2 * full):
+        mac(u)
+    for j in range(4):
+        receive(full + 1, j)
+    mac(far)
+
+    bn[...] = acc[:, 0:gw].astype(jnp.bfloat16)
+    cn[...] = acc[:, gw:2 * gw].astype(jnp.bfloat16)
+    at = 2 * gw
+    dt_sum = acc[:, at:at + heads] + acc[:, at + LANES + heads:at + LANES + 2 * heads] + bias
+    dtn[...] = jnp.maximum(dt_sum, 0.0) + jnp.log1p(jnp.exp(-jnp.abs(dt_sum)))
+    x_load.wait()
+    local_states(False, dims, len_ref, xv, bn, dtn, decay_ref, work, *kept[0][2:])
+    exchange(0)
+    combine(0)
+    block(False, 0)
+    for back in range(2):
+        kx_copy(back).wait_recv()
+
+    def tick(t, _):
+        for back in range(2):
+            i = t - ((nz - 1 - zpos) if back else zpos) * Z_LAG
+
+            @pl.when((i >= 0) & (i < half_pairs))
+            def _(back=back, i=i):
+                relay(back, i)
+
+            late = i - CORE_LAG
+
+            @pl.when((late >= 0) & (late < half_pairs))
+            def _(back=back, late=late):
+                settle(back, late)
+
+        return 0
+
+    lax.fori_loop(0, half_pairs + CORE_LAG + (nz - 1) * Z_LAG, tick, 0)
+
+    for j in range(2):
+        cross(j).wait_send()
+    for k in range(1, half_ring + 1):
+        for d in range(2):
+            for j in range(4):
+                if k <= full or (j < 2) == (d == 0):
+                    ring(d, k, j).wait_send()
+    for u in range(far + 1):
+        for j in range(4):
+            side(u, j).wait_send()
+    for back in range(2):
+        remote(kv[back], ksib[back], k_s.at[back], k_r.at[back], seq=partner).wait_send()
+        kx_copy(back).wait_send()
+
+        def drain(i, _, back=back):
+            remote(lout[back].at[i], lin[back].at[i], l_s.at[back, i], l_r.at[back, i], seq=partner).wait_send()
+            x_copy(back, i).wait_send()
+            e_copy(back, i).wait_send()
+
+            @pl.when(zpos != (0 if back else nz - 1))
+            def _():
+                z_copy(back, i).wait_send()
+
+            out_copy(back, i).wait()
+            out_copy(back, half_pairs + i).wait()
+            return 0
+
+        lax.fori_loop(0, half_pairs, drain, 0)
+
+
+def fused(hidden, values, seg_next, proj_bc, proj_dt, dt_bias, decay_rate, skip_gain,
+          bc_prev, dt_prev, seg_prev, grad, gw):
+    count = lax.axis_size("seq")
+    tokens, heads = dt_prev.shape
+    width = values.shape[1]
+    dims = (tokens // SPAN, heads, gw // LANES, width // heads)
+    npair = width // LANES
+    half_pairs = npair // 2
+    n = count // 2
+    f32, bf16 = jnp.float32, jnp.bfloat16
+    dma = pltpu.SemaphoreType.DMA
+    wrows = proj_bc.shape[0]
+    packed = wrows + LANES * LANES // (2 * gw)
+    nblocks = dims[0]
+    work = [pltpu.VMEM((tokens, heads), f32), pltpu.VMEM((nblocks, heads, SPAN), f32),
+            pltpu.VMEM((nblocks, heads, SPAN), f32), pltpu.VMEM((tokens, heads), f32)]
+    kept = [pltpu.VMEM(s, f32) for s in ((npair, tokens, LANES), (npair, tokens, LANES),
+                                         (nblocks + 1, npair, LANES, LANES), (nblocks + 1, npair, 1, LANES))]
+    box = [pltpu.VMEM((half_pairs, LANES, LANES), bf16)] * 2
+    gain = [pltpu.VMEM((npair, LANES), f32)] * 2
+    half_gain = [pltpu.VMEM((half_pairs, LANES), f32)] * 2
+    hbm = pl.BlockSpec(memory_space=pl.ANY)
+    steps = n // 2
+    return pl.pallas_call(
+        functools.partial(fused_kernel, count, dims),
+        out_shape=[jax.ShapeDtypeStruct(values.shape, bf16)] * 2,
+        in_specs=[SM] * 2 + [VM] * 5 + [hbm] * 5,
+        out_specs=[hbm] * 2,
+        scratch_shapes=[
+            pltpu.VMEM((tokens, hidden.shape[1]), bf16),
+            pltpu.VMEM((n, 4, packed, 2 * gw), bf16),
+            pltpu.VMEM((packed, 2 * gw), bf16),
+            pltpu.VMEM((tokens, width), bf16), pltpu.VMEM((tokens, width), bf16),
+            *[pltpu.VMEM((tokens, gw), bf16)] * 4,
+            pltpu.VMEM((tokens, 2 * gw + 2 * LANES), f32),
+            pltpu.VMEM((tokens, heads), f32), pltpu.VMEM((tokens, heads), f32),
+            pltpu.VMEM((1, heads), f32), pltpu.VMEM((1, heads), f32),
+            *work, *work, *kept, *kept, *box * 8, *gain * 2, *half_gain * 2,
+            dma((9,)), dma((2, steps, 4)), dma((2, steps, 4)), dma((n, 4)), dma((n, 4)),
+            dma((2,)), dma((2,)), dma((2, half_pairs)), dma((2, half_pairs)), dma((4,)), dma((4,)),
+            dma((2, half_pairs)), dma((2, half_pairs)), dma((2, half_pairs)), dma((2, half_pairs)),
+            dma((2, half_pairs)), dma((2, half_pairs)), dma((2, npair)),
+        ],
+        compiler_params=pltpu.CompilerParams(
+            collective_id=2, has_side_effects=True, vmem_limit_bytes=67_043_328),
+        name="fused",
+    )(seg_next, seg_prev, dt_bias[None], decay_rate[None], skip_gain[None], proj_dt, dt_prev.T,
+      hidden, values, proj_bc, bc_prev, grad)
+
+
 def body(
     hidden_next, values_next, seg_next, proj_bc, proj_dt, dt_bias, decay_rate, skip_gain,
     bc_prev, dt_prev, seg_prev, grad_prev,
@@ -445,6 +863,11 @@
     rows_dev = proj_bc.shape[0]
     half = bc_width // 2
     gw = groups_dev * state_dim
+
+    if fsdp_count == 2 and seq_count % 4 == 0 and seq_count >= 8 and heads_all == LANES \
+            and rows_dev == 2 * LANES and groups_dev * per_group == heads_dev:
+        return fused(hidden_next, values_next, seg_next, proj_bc, proj_dt, dt_bias, decay_rate,
+                     skip_gain, bc_prev, dt_prev, seg_prev, grad_prev, gw)
 
     blocks = []
     for f in range(fsdp_count):

time: 154 us -> 108 us (0.70)
  Pallas kernels: 136 us -> 103 us
  local copies, waits for them, and re-layouts: 15.8 us -> 4.6 us
    pallas_call x2 -> x1, Pallas kernels: 136 us -> 103 us  [fused(): pl.pallas_call(functools.partial(fused_kernel, count, dims), out_shape=[j...]
    unnamed x13 -> x4, local copies, waits for them, and re-layouts: 12 us -> 4.6 us
    dynamic_slice x2 -> x0, local copies, waits for them, and re-layouts: 1.54 us -> none  [the longest x1 0.81 us: body(): lax.dynamic_slice_in_dim(bc_prev, half + first_group * state_dim, gw, 1)]
where the time goes in v1:
time: 108 us
  Pallas kernels  103 us (95%)
  local copies, waits for them, and re-layouts  4.6 us (4%)
    pallas_call x1, Pallas kernels, fused(): pl.pallas_call(functools.partial(fused_kernel, count, dims), out_shape=[j...  103 us
    unnamed x4, local copies, waits for them, and re-layouts  4.6 us

profile of v1, /device:TPU:0, one launch (start us, length us, event | category | flops | bytes accessed | tf_op | source)
XLA Modules:
  0.0 108.3 jit_solution(18265982169479623560)
XLA Ops:
  0.6 103.1 %fused.1 = (bf16[256,4096]{1,0:T(8,128)(2,1)}, bf16[256,4096]{1,0:T(8,128)(2,1)}) custom-call(s32[4]{0:T(128)} %len_ref.1, s32[4]{0:T(128)} %lenb_ref.1, f32[1,128]{1,0:T(1,128)} %bitcast.5, f32[1,128]{1,0:T(1,128)} %bitcast.6, f32[1,128]{1,0:T(1,128)} %bitcast.7, bf16[256,128]{1,0:T(8,128)(2,1)} %pdt_ref.1, f32[64,256]{1,0:T(8,128)} %bitcast.4, ...), custom_call_target="tpu_custom_call" | custom-call | tf_op jit(solution)/shard_map/fused/pallas_call | solution.py:820
  103.7 0.0 copy-start
  103.7 3.3 %copy.16 = bf16[256,4096]{1,0:T(8,128)(2,1)} copy(bf16[256,4096]{1,0:T(8,128)(2,1)} %get-tuple-element.4) | data formatting | bytes 4194304
  107.0 0.0 copy-done
  107.0 1.3 %copy.17 = bf16[256,4096]{1,0:T(8,128)(2,1)} copy(bf16[256,4096]{1,0:T(8,128)(2,1)S(1)} %copy-done) | data formatting | bytes 4194304
Async XLA Ops:
  103.7 3.3 %copy-start = (bf16[256,4096]{1,0:T(8,128)(2,1)S(1)}, bf16[256,4096]{1,0:T(8,128)(2,1)}, u32[]{:S(2)}) copy-start(bf16[256,4096]{1,0:T(8,128)(2,1)} %get-tuple-element.5) | copy-start | bytes 6291460

commit v2 on v1

--- a/solution.py
+++ b/solution.py
@@ -429,18 +429,20 @@
 
 Z_LAG = 4
 CORE_LAG = 3
+BATCH = 4
+EARLY = 6
 
 
 def fused_kernel(count, dims, len_ref, lenb_ref, bias_in, decay_in, skip_in, pdt_ref, dtt_ref,
                  h_hbm, x_hbm, w_hbm, bcp_hbm, g_hbm, out_hbm, grad_hbm,
-                 hid, held, yout, xv, gv, bp, cp, bn, cn, acc, dtn, dtp, decay_ref, skip_ref,
+                 hid, held_b, held_c, yout_b, yout_c, xv, gv, bp, cp, bn, cn, acc, dtn, dtp, decay_ref, skip_ref,
                  *scratch):
     work, work_b = scratch[:4], scratch[4:8]
     kept = (scratch[8:12], scratch[12:16])
-    lout, lin, xout, xin, zout, zin, eout, ein, kv, ksib, kxo, kxi = (
-        (scratch[16 + 2 * i], scratch[17 + 2 * i]) for i in range(12))
+    lout, lin, xout, xin, zout, zin, eout, ein, eown, kv, ksib, kxo, kxi = (
+        (scratch[16 + 2 * i], scratch[17 + 2 * i]) for i in range(13))
     (ld, ring_s, ring_r, side_s, side_r, y_s, y_r, l_s, l_r, k_s, k_r, c_s, c_r, z_s, z_r,
-     e_s, e_r, o_sem) = scratch[40:]
+     e_s, e_r, o_sem) = scratch[42:]
     nblocks, heads, groups, head_dim = dims
     npair = heads * head_dim // LANES
     pair_group = npair // groups
@@ -454,7 +456,6 @@
     far = 2 * full + 1
     gw = groups * LANES
     wrows = w_hbm.shape[0]
-    prow = held.shape[2] // 2
     r = jnp.where(xpos == 0, zpos, n - 1 - zpos)
 
     def chip_at(pos):
@@ -474,10 +475,10 @@
 
     w_half = w_hbm.shape[1] // 2
     w_loads = [
-        load(w_hbm.at[:, at_cols(f * gw)], held.at[chip, own, 0:wrows, 0:gw], 0),
-        load(w_hbm.at[:, at_cols(w_half + f * gw)], held.at[chip, own, 0:wrows, gw:2 * gw], 1),
-        load(w_hbm.at[:, at_cols((1 - f) * gw)], yout.at[0:wrows, 0:gw], 2),
-        load(w_hbm.at[:, at_cols(w_half + (1 - f) * gw)], yout.at[0:wrows, gw:2 * gw], 3),
+        load(w_hbm.at[:, at_cols(f * gw)], held_b.at[chip, own, 0:wrows, :], 0),
+        load(w_hbm.at[:, at_cols((1 - f) * gw)], yout_b.at[0:wrows, :], 1),
+        load(w_hbm.at[:, at_cols(w_half + f * gw)], held_c.at[chip, own, :, :], 2),
+        load(w_hbm.at[:, at_cols(w_half + (1 - f) * gw)], yout_c, 3),
     ]
     b_loads = [
         load(g_hbm, gv, 4),
@@ -508,12 +509,12 @@
     pack1 = jnp.where(lane < heads, pltpu.roll(top, heads, 1), low)
     mine = jnp.where(f == 0, pack0, pack1).astype(jnp.bfloat16)
     theirs = jnp.where(f == 0, pack1, pack0).astype(jnp.bfloat16)
-    strips = 2 * gw // LANES
+    strips = gw // LANES
     strip = LANES // strips
     for k in range(strips):
         lanes = slice(k * LANES, (k + 1) * LANES)
-        held[chip, own, wrows:wrows + strip, lanes] = mine[k * strip:(k + 1) * strip, :]
-        yout[wrows:wrows + strip, lanes] = theirs[k * strip:(k + 1) * strip, :]
+        held_b[chip, own, wrows:wrows + strip, lanes] = mine[k * strip:(k + 1) * strip, :]
+        yout_b[wrows:wrows + strip, lanes] = theirs[k * strip:(k + 1) * strip, :]
     decay_ref[...] = jnp.where(f == 0, decay_in[:, 0:heads], decay_in[:, heads:2 * heads])
     skip_ref[...] = jnp.where(f == 0, skip_in[:, 0:heads], skip_in[:, heads:2 * heads])
     bias = jnp.where(f == 0, bias_in[:, 0:heads], bias_in[:, heads:2 * heads])
@@ -524,12 +525,9 @@
     for copy in w_loads:
         copy.wait()
 
-    def rows_of(j):
-        return pl.ds((j % 2) * prow, prow)
-
     def piece(where, j, mine=True):
         base = (core if mine else 1 - core) * 2
-        return held.at[where, base + (f if j < 2 else 1 - f), rows_of(j), :]
+        return (held_b if j < 2 else held_c).at[where, base + (f if j % 2 == 0 else 1 - f)]
 
     def remote(src, dst, s, rv, **peer):
         return pltpu.make_async_remote_copy(src_ref=src, dst_ref=dst, send_sem=s, recv_sem=rv,
@@ -548,48 +546,53 @@
         ref = piece(chip_of(u), j, not arrived)
         return remote(ref, ref, side_s.at[u, j], side_r.at[u, j], seq=partner)
 
-    def cross(j, arrived=False):
-        dst = held.at[chip, other, rows_of(j), :]
-        dst = dst if arrived else held.at[chip, own, rows_of(j), :]
-        return remote(yout.at[rows_of(j), :], dst, y_s.at[j], y_r.at[j], fsdp=1 - f)
+    def cross(kind, arrived=False):
+        ref = held_c if kind else held_b
+        return remote(yout_c if kind else yout_b, ref.at[chip, other if arrived else own],
+                      y_s.at[kind], y_r.at[kind], fsdp=1 - f)
 
     def begin(j):
         ring(0, 1, j).start()
         ring(1, 1, j).start()
         side(0, j).start()
 
-    for j in range(2):
-        cross(j).start()
-        begin(j)
-
-    def receive(k, j):
+    for kind in range(2):
+        cross(kind).start()
+        begin(2 * kind)
+
+    def receive(k, kind, second=False):
         for d in range(2):
-            if k > full and (j < 2) != (d == 0):
+            if k > full and second:
                 continue
+            j = 2 * kind + ((1 - d if second else d) if k > 1 or kind else int(second))
             ring(d, k, j, True).wait_recv()
-            if k < full or (k == full and (j < 2) == (d == 0)):
+            if k < full or (k == full and j % 2 == d):
                 ring(d, k + 1, j).start()
             side(far if k > full else (k if d == 0 else full + k), j).start()
 
-    def mac(u, first=False):
-        for j in range(4):
+    wide = 4 * wrows
+
+    def add(at, value, first):
+        cols = slice(at, at + value.shape[1])
+        acc[:, cols] = value if first else acc[:, cols] + value
+
+    def mac(u, kind, first=False):
+        for j in (2 * kind, 2 * kind + 1):
             side(u, j, True).wait_recv()
         q = chip_of(u)
-        wide = 4 * wrows
         left = hid[:, pl.ds(pl.multiple_of(q * wide, wide), wide)]
-        main = jnp.dot(left, jnp.concatenate([held[q, s, 0:wrows, :] for s in range(4)], axis=0),
-                       preferred_element_type=jnp.float32)
-        packs = jnp.concatenate(
-            [held[q, s, wrows:wrows + strip, k * LANES:(k + 1) * LANES]
-             for s in range(4) for k in range(strips)], axis=0)
-        parts = [jnp.dot(jnp.concatenate([left[:, s * wrows + o:s * wrows + o + LANES] for s in range(4)], axis=1),
-                         packs, preferred_element_type=jnp.float32) for o in (0, LANES)]
-        for at, value in ((0, main), (2 * gw, parts[0]), (2 * gw + LANES, parts[1])):
-            cols = slice(at, at + value.shape[1])
-            acc[:, cols] = value if first else acc[:, cols] + value
-
-    def my_half(back):
-        return core * half_pairs
+        ref = held_c if kind else held_b
+        add(gw + 2 * LANES if kind else 0,
+            jnp.dot(left, jnp.concatenate([ref[q, s, 0:wrows, :] for s in range(4)], axis=0),
+                    preferred_element_type=jnp.float32), first)
+        if kind == 0:
+            packs = jnp.concatenate(
+                [held_b[q, s, wrows:wrows + strip, k * LANES:(k + 1) * LANES]
+                 for s in range(4) for k in range(strips)], axis=0)
+            for o in range(2):
+                part = jnp.concatenate(
+                    [left[:, s * wrows + o * LANES:s * wrows + (o + 1) * LANES] for s in range(4)], axis=1)
+                add(gw + o * LANES, jnp.dot(part, packs, preferred_element_type=jnp.float32), first)
 
     def exchange(back):
         pre, keep = kept[back][2:]
@@ -610,6 +613,15 @@
     def lead_x(back):
         return (xpos == 1) if back else (xpos == 0)
 
+    def ends(back):
+        return (zpos == 0) if back else (zpos == nz - 1)
+
+    def gives(back):
+        return jnp.logical_not(ends(back)) | lead_x(back)
+
+    def takes(back):
+        return jnp.logical_not(ends(back) & lead_x(back))
+
     def row(ref, i):
         return ref[pl.ds(i, 1), :]
 
@@ -620,11 +632,18 @@
         return remote(kxo[back], kxi[back], k_s.at[2 + back], k_r.at[2 + back], seq=xpeer)
 
     def combine(back):
-        pre = kept[back][2]
         rows = pl.ds(pl.multiple_of(core * half_pairs, half_pairs), half_pairs)
         remote(kv[back], ksib[back], k_s.at[back], k_r.at[back], seq=partner).wait_recv()
         kxo[back][...] = kv[back][rows, :] * ksib[back][rows, :]
-        kx_copy(back).start()
+        sends = gives(back)
+
+        @pl.when(sends)
+        def _():
+            kx_copy(back).start()
+
+    def combine_part(back, start, stop):
+        pre = kept[back][2]
+        sends = gives(back)
 
         def put(i, _):
             g = core * half_pairs + i
@@ -633,10 +652,14 @@
             total = (pre[nblocks, g] * jnp.where(lead, row(ksib[back], g), 1.0)
                      + lin[back][i].astype(jnp.float32) * jnp.where(lead, 1.0, row(kv[back], g)))
             xout[back][i] = total.astype(jnp.bfloat16)
-            x_copy(back, i).start()
+
+            @pl.when(sends)
+            def _():
+                x_copy(back, i).start()
+
             return 0
 
-        lax.fori_loop(0, half_pairs, put, 0)
+        lax.fori_loop(start, stop, put, 0)
 
     def z_copy(back, i):
         return remote(zout[back].at[i], zin[back].at[i], z_s.at[back, i], z_r.at[back, i],
@@ -645,36 +668,49 @@
     def e_copy(back, i):
         return remote(eout[back].at[i], ein[back].at[i], e_s.at[back, i], e_r.at[back, i], seq=partner)
 
-    def out_copy(back, c):
-        cols = pl.ds(pl.multiple_of(c * LANES, LANES), LANES)
+    def out_copy(back, k):
+        cols = pl.ds(pl.multiple_of(k * BATCH * LANES, LANES), BATCH * LANES)
         src, dst = (gv, grad_hbm) if back else (xv, out_hbm)
-        return pltpu.make_async_copy(src.at[:, cols], dst.at[:, cols], o_sem.at[back, c])
-
-    def finish(back, c, state):
+        return pltpu.make_async_copy(src.at[:, cols], dst.at[:, cols], o_sem.at[back, k])
+
+    def finish(back, c0, states, i0):
         ins, fx, pre, keep = kept[back]
         vec, out = (bp, gv) if back else (cn, xv)
-        cols = pl.ds(pl.multiple_of(c * LANES, LANES), LANES)
-        gl = pl.ds(pl.multiple_of((c // pair_group) * LANES, LANES), LANES)
+        gl = pl.ds(pl.multiple_of((c0 // pair_group) * LANES, LANES), LANES)
         for step in range(nblocks):
             b = nblocks - 1 - step if back else step
             rows = slice(b * SPAN, (b + 1) * SPAN)
-            entering = state if step == 0 else keep[step, c] * state + pre[step, c]
-            y = jnp.dot(vec[rows, gl], entering.astype(jnp.bfloat16), preferred_element_type=jnp.float32)
-            out[rows, cols] = (ins[c, rows, :] + fx[c, rows, :] * y).astype(jnp.bfloat16)
-        out_copy(back, c).start()
+            for k in range(0, BATCH, 2):
+                entering = []
+                for c, i in ((c0 + k, i0 + k), (c0 + k + 1, i0 + k + 1)):
+                    state = states[i]
+                    if step > 0:
+                        state = (keep[step, c] * state.astype(jnp.float32) + pre[step, c]).astype(jnp.bfloat16)
+                    entering.append(state)
+                y = jnp.dot(vec[rows, gl], jnp.concatenate(entering, axis=1), preferred_element_type=jnp.float32)
+                for m in range(2):
+                    c = c0 + k + m
+                    cols = pl.ds(pl.multiple_of(c * LANES, LANES), LANES)
+                    part = y[:, m * LANES:(m + 1) * LANES]
+                    out[rows, cols] = (ins[c, rows, :] + fx[c, rows, :] * part).astype(jnp.bfloat16)
+        out_copy(back, c0 // BATCH).start()
 
     def relay(back, i):
         pre = kept[back][2]
         g = core * half_pairs + i
         z_first, z_last = (zpos == nz - 1, zpos == 0) if back else (zpos == 0, zpos == nz - 1)
-        x_copy(back, i).wait_recv()
+
+        @pl.when(takes(back))
+        def _():
+            x_copy(back, i).wait_recv()
 
         @pl.when(jnp.logical_not(z_first))
         def _():
             z_copy(back, i).wait_recv()
 
         k_own, k_peer = row(kxo[back], i), row(kxi[back], i)
-        l_own, l_peer = xout[back][i].astype(jnp.float32), xin[back][i].astype(jnp.float32)
+        l_own = xout[back][i].astype(jnp.float32)
+        l_peer = jnp.where(takes(back), xin[back][i].astype(jnp.float32), 0.0)
         state = jnp.where(z_first, 0.0, zin[back][i].astype(jnp.float32))
         lead = lead_x(back)
         zout[back][i] = (k_own * k_peer * state + l_own * jnp.where(lead, k_peer, 1.0)
@@ -691,21 +727,13 @@
         after = k_lead * state + l_lead
         eout[back][i] = jnp.where(head, after, state).astype(jnp.bfloat16)
         e_copy(back, i).start()
-        finish(back, g, jnp.where(head, state, after))
+        eown[back][i] = jnp.where(head, state, after).astype(jnp.bfloat16)
 
     def settle(back, i):
-        e_copy(back, i).wait_recv()
-        finish(back, (1 - core) * half_pairs + i, ein[back][i].astype(jnp.float32))
-
-    for copy in b_loads:
-        copy.wait()
-    local_states(True, dims, lenb_ref, gv, cp, dtp, decay_ref, work_b, *kept[1][2:])
-    for j in range(2):
-        cross(j, True).wait_recv()
-        begin(j + 2)
-    exchange(1)
-    receive(1, 0)
-    receive(1, 1)
+        for k in range(BATCH):
+            e_copy(back, i + k).wait_recv()
+        finish(back, core * half_pairs + i, eown[back], i)
+        finish(back, (1 - core) * half_pairs + i, ein[back], i)
 
     def block(back, b):
         if back:
@@ -713,38 +741,71 @@
         else:
             in_block(False, dims, len_ref, xv, cn, bn, dtn, skip_ref, work, *kept[0][:2])
 
+    for copy in b_loads:
+        copy.wait()
+    local_states(True, dims, lenb_ref, gv, cp, dtp, decay_ref, work_b, *kept[1][2:])
+    for kind in range(2):
+        cross(kind, True).wait_recv()
+        begin(2 * kind + 1)
+    receive(1, 0)
+    exchange(1)
     block(True, 0)
-    receive(1, 2)
-    receive(1, 3)
+    receive(1, 0, True)
+    receive(1, 1)
     block(True, 1)
     h_load.wait()
+    mac(0, 0, True)
+    c_next = [(k, second) for k in range(1, full + 1) for second in (False, True)][1:]
     for k in range(2, full + 1):
-        for j in range(4):
-            receive(k, j)
-            if j == 1 and k == full:
-                combine(1)
+        receive(k, 0)
+        receive(k, 0, True)
         if k == 2:
-            mac(0, True)
+            mac(0, 1, True)
         for u in (k - 1, full + k - 1):
-            mac(u)
+            mac(u, 0)
+        for _ in range(2 if k == full else 1):
+            step, second = c_next.pop(0)
+            receive(step, 1, second)
     for u in (full, 2 * full):
-        mac(u)
-    for j in range(4):
-        receive(full + 1, j)
-    mac(far)
-
+        mac(u, 0)
+    receive(full + 1, 0)
+    mac(far, 0)
+    at = gw
     bn[...] = acc[:, 0:gw].astype(jnp.bfloat16)
-    cn[...] = acc[:, gw:2 * gw].astype(jnp.bfloat16)
-    at = 2 * gw
     dt_sum = acc[:, at:at + heads] + acc[:, at + LANES + heads:at + LANES + 2 * heads] + bias
     dtn[...] = jnp.maximum(dt_sum, 0.0) + jnp.log1p(jnp.exp(-jnp.abs(dt_sum)))
+    while len(c_next) > 1:
+        step, second = c_next.pop(0)
+        receive(step, 1, second)
+    early = jnp.where(zpos == 0, EARLY, half_pairs)
+    combine(1)
+    combine_part(1, 0, early)
     x_load.wait()
     local_states(False, dims, len_ref, xv, bn, dtn, decay_ref, work, *kept[0][2:])
     exchange(0)
+    for step, second in c_next:
+        receive(step, 1, second)
+    for k in range(1, full):
+        for u in (k, full + k):
+            mac(u, 1)
     combine(0)
+    combine_part(0, 0, half_pairs)
+    combine_part(1, early, half_pairs)
+    for u in (full, 2 * full):
+        mac(u, 1)
+    receive(full + 1, 1)
+    mac(far, 1)
+    cn[...] = acc[:, gw + 2 * LANES:].astype(jnp.bfloat16)
     block(False, 0)
     for back in range(2):
-        kx_copy(back).wait_recv()
+        @pl.when(takes(back))
+        def _(back=back):
+            kx_copy(back).wait_recv()
+
+        @pl.when(jnp.logical_not(takes(back)))
+        def _(back=back):
+            kxi[back][...] = jnp.zeros_like(kxi[back])
+
 
     def tick(t, _):
         for back in range(2):
@@ -754,11 +815,12 @@
             def _(back=back, i=i):
                 relay(back, i)
 
-            late = i - CORE_LAG
-
-            @pl.when((late >= 0) & (late < half_pairs))
+        for back in range(2):
+            late = t - ((nz - 1 - zpos) if back else zpos) * Z_LAG - CORE_LAG
+
+            @pl.when((late >= 0) & (late < half_pairs) & (late % BATCH == BATCH - 1))
             def _(back=back, late=late):
-                settle(back, late)
+                settle(back, late - (BATCH - 1))
 
         return 0
 
@@ -769,29 +831,37 @@
     for k in range(1, half_ring + 1):
         for d in range(2):
             for j in range(4):
-                if k <= full or (j < 2) == (d == 0):
+                if k <= full or j % 2 == d:
                     ring(d, k, j).wait_send()
     for u in range(far + 1):
         for j in range(4):
             side(u, j).wait_send()
     for back in range(2):
         remote(kv[back], ksib[back], k_s.at[back], k_r.at[back], seq=partner).wait_send()
-        kx_copy(back).wait_send()
-
-        def drain(i, _, back=back):
+        given = gives(back)
+
+        @pl.when(given)
+        def _(back=back):
+            kx_copy(back).wait_send()
+
+        def drain(i, _, back=back, given=given):
             remote(lout[back].at[i], lin[back].at[i], l_s.at[back, i], l_r.at[back, i], seq=partner).wait_send()
-            x_copy(back, i).wait_send()
+
+            @pl.when(given)
+            def _():
+                x_copy(back, i).wait_send()
+
             e_copy(back, i).wait_send()
 
             @pl.when(zpos != (0 if back else nz - 1))
             def _():
                 z_copy(back, i).wait_send()
 
-            out_copy(back, i).wait()
-            out_copy(back, half_pairs + i).wait()
             return 0
 
         lax.fori_loop(0, half_pairs, drain, 0)
+        for k in range(npair // BATCH):
+            out_copy(back, k).wait()
 
 
 def fused(hidden, values, seg_next, proj_bc, proj_dt, dt_bias, decay_rate, skip_gain,
@@ -806,7 +876,7 @@
     f32, bf16 = jnp.float32, jnp.bfloat16
     dma = pltpu.SemaphoreType.DMA
     wrows = proj_bc.shape[0]
-    packed = wrows + LANES * LANES // (2 * gw)
+    packed = wrows + LANES * LANES // gw
     nblocks = dims[0]
     work = [pltpu.VMEM((tokens, heads), f32), pltpu.VMEM((nblocks, heads, SPAN), f32),
             pltpu.VMEM((nblocks, heads, SPAN), f32), pltpu.VMEM((tokens, heads), f32)]
@@ -817,31 +887,60 @@
     half_gain = [pltpu.VMEM((half_pairs, LANES), f32)] * 2
     hbm = pl.BlockSpec(memory_space=pl.ANY)
     steps = n // 2
-    return pl.pallas_call(
+    staged = pl.pallas_call(
         functools.partial(fused_kernel, count, dims),
         out_shape=[jax.ShapeDtypeStruct(values.shape, bf16)] * 2,
         in_specs=[SM] * 2 + [VM] * 5 + [hbm] * 5,
         out_specs=[hbm] * 2,
         scratch_shapes=[
             pltpu.VMEM((tokens, hidden.shape[1]), bf16),
-            pltpu.VMEM((n, 4, packed, 2 * gw), bf16),
-            pltpu.VMEM((packed, 2 * gw), bf16),
+            pltpu.VMEM((n, 4, packed, gw), bf16), pltpu.VMEM((n, 4, wrows, gw), bf16),
+            pltpu.VMEM((packed, gw), bf16), pltpu.VMEM((wrows, gw), bf16),
             pltpu.VMEM((tokens, width), bf16), pltpu.VMEM((tokens, width), bf16),
             *[pltpu.VMEM((tokens, gw), bf16)] * 4,
             pltpu.VMEM((tokens, 2 * gw + 2 * LANES), f32),
             pltpu.VMEM((tokens, heads), f32), pltpu.VMEM((tokens, heads), f32),
             pltpu.VMEM((1, heads), f32), pltpu.VMEM((1, heads), f32),
-            *work, *work, *kept, *kept, *box * 8, *gain * 2, *half_gain * 2,
+            *work, *work, *kept, *kept, *box * 9, *gain * 2, *half_gain * 2,
             dma((9,)), dma((2, steps, 4)), dma((2, steps, 4)), dma((n, 4)), dma((n, 4)),
             dma((2,)), dma((2,)), dma((2, half_pairs)), dma((2, half_pairs)), dma((4,)), dma((4,)),
             dma((2, half_pairs)), dma((2, half_pairs)), dma((2, half_pairs)), dma((2, half_pairs)),
-            dma((2, half_pairs)), dma((2, half_pairs)), dma((2, npair)),
+            dma((2, half_pairs)), dma((2, half_pairs)), dma((2, npair // BATCH)),
         ],
         compiler_params=pltpu.CompilerParams(
             collective_id=2, has_side_effects=True, vmem_limit_bytes=67_043_328),
         name="fused",
     )(seg_next, seg_prev, dt_bias[None], decay_rate[None], skip_gain[None], proj_dt, dt_prev.T,
       hidden, values, proj_bc, bc_prev, grad)
+    chunk = pltpu.VMEM((tokens, width), bf16)
+    return pl.pallas_call(
+        hand_over,
+        out_shape=[jax.ShapeDtypeStruct(values.shape, bf16)] * 2,
+        in_specs=[hbm] * 2,
+        out_specs=[hbm] * 2,
+        scratch_shapes=[chunk, chunk, dma((2, HAND_PARTS)), dma((2, HAND_PARTS))],
+        name="hand_over",
+    )(*staged)
+
+
+HAND_PARTS = 8
+
+
+def hand_over(a_in, b_in, a_out, b_out, a_buf, b_buf, in_sem, out_sem):
+    part = a_in.shape[0] // HAND_PARTS
+    reads, writes = [], []
+    for p in range(HAND_PARTS):
+        rows = pl.ds(p * part, part)
+        for k, (src, buf, dst) in enumerate(((a_in, a_buf, a_out), (b_in, b_buf, b_out))):
+            reads.append(pltpu.make_async_copy(src.at[rows, :], buf.at[rows, :], in_sem.at[k, p]))
+            writes.append(pltpu.make_async_copy(buf.at[rows, :], dst.at[rows, :], out_sem.at[k, p]))
+    for copy in reads:
+        copy.start()
+    for read, write in zip(reads, writes):
+        read.wait()
+        write.start()
+    for copy in writes:
+        copy.wait()
 
 
 def body(

time: 108 us -> 93.1 us (0.86); the launches traced: 108 us -> 91.6 us
  Pallas kernels: 103 us -> 90.8 us
  local copies, waits for them, and re-layouts: 4.6 us -> 0 us
    pallas_call x1, Pallas kernels: 103 us -> 87 us  [fused(): pl.pallas_call(functools.partial(fused_kernel, count, dims), out_shape=[j...]
    unnamed x4 -> x0, local copies, waits for them, and re-layouts: 4.6 us -> none
    pallas_call x0 -> x1, Pallas kernels: none -> 3.85 us  [fused(): pl.pallas_call(hand_over, out_shape=[jax.ShapeDtypeStruct(values.shape, b...]
where the time goes in v2:
time: 93.1 us; the launch traced here: 91.6 us
  Pallas kernels  90.8 us (98%)
    pallas_call x1, Pallas kernels, fused(): pl.pallas_call(functools.partial(fused_kernel, count, dims), out_shape=[j...  87 us
    pallas_call x1, Pallas kernels, fused(): pl.pallas_call(hand_over, out_shape=[jax.ShapeDtypeStruct(values.shape, b...  3.85 us

profile of v2, /device:TPU:0, one launch (start us, length us, event | category | flops | bytes accessed | tf_op | source)
XLA Modules:
  0.0 91.6 jit_solution(5716688453466442930)
XLA Ops:
  0.6 87.0 %fused.1 = (bf16[256,4096]{1,0:T(8,128)(2,1)}, bf16[256,4096]{1,0:T(8,128)(2,1)}) custom-call(s32[4]{0:T(128)} %len_ref.1, s32[4]{0:T(128)} %lenb_ref.1, f32[1,128]{1,0:T(1,128)} %bitcast.5, f32[1,128]{1,0:T(1,128)} %bitcast.6, f32[1,128]{1,0:T(1,128)} %bitcast.7, bf16[256,128]{1,0:T(8,128)(2,1)} %pdt_ref.1, f32[64,256]{1,0:T(8,128)} %bitcast.4, ...), custom_call_target="tpu_custom_call" | custom-call | tf_op jit(solution)/shard_map/fused/pallas_call | solution.py:890
  87.6 3.9 %hand_over.1 = (bf16[256,4096]{1,0:T(8,128)(2,1)}, bf16[256,4096]{1,0:T(8,128)(2,1)}) custom-call(bf16[256,4096]{1,0:T(8,128)(2,1)} %get-tuple-element.4.a_in, bf16[256,4096]{1,0:T(8,128)(2,1)} %get-tuple-element.5.b_in), custom_call_target="tpu_custom_call" | custom-call | tf_op jit(solution)/shard_map/hand_over/pallas_call | solution.py:916

commit v3 on v2

--- a/solution.py
+++ b/solution.py
@@ -38,7 +38,7 @@
     return seg_of
 
 
-def local_states(back, dims, len_ref, x_ref, q_ref, dt_ref, decay_ref, work, pre, keep):
+def local_states(back, dims, len_ref, x_ref, q_ref, dt_ref, decay_ref, work, pre, keep, part=None):
     nblocks, heads, groups, head_dim = dims
     cum_s, cum_t, dt_t, fout_s = work
     npair = heads * head_dim // LANES
@@ -48,10 +48,11 @@
     dim0 = lax.broadcasted_iota(jnp.int32, (SPAN, SPAN), 0)
     dim1 = lax.broadcasted_iota(jnp.int32, (SPAN, SPAN), 1)
     tril = (dim0 >= dim1).astype(jnp.float32)
-    for c in range(npair):
+    steps = range(nblocks) if part is None else part
+    for c in range(npair if 0 in steps else 0):
         pre[0, c] = jnp.zeros((LANES, LANES), jnp.float32)
         keep[0, c] = jnp.ones((1, LANES), jnp.float32)
-    for step in range(nblocks):
+    for step in steps:
         b = nblocks - 1 - step if back else step
         rows = slice(b * SPAN, (b + 1) * SPAN)
         dt = dt_ref[rows, :]
@@ -80,7 +81,8 @@
             keep[step + 1, c] = wide * keep[step, c]
 
 
-def in_block(back, dims, len_ref, x_ref, p_ref, q_ref, dt_ref, skip_ref, work, inside, fexp, span=None):
+def in_block(back, dims, len_ref, x_ref, p_ref, q_ref, dt_ref, skip_ref, work, inside, fexp, span=None,
+             only=None):
     nblocks, heads, groups, head_dim = dims
     cum_s, cum_t, dt_t, fout_s = work
     npair = heads * head_dim // LANES
@@ -102,7 +104,7 @@
         cum = cum_s[rows, :]
         dt = dt_ref[rows, :]
         f_out = fout_s[rows, :]
-        for g in range(groups):
+        for g in range(groups) if only is None else (only,):
             gl = slice(g * LANES, (g + 1) * LANES)
             score = lax.dot_general(p_ref[rows, gl], q_ref[rows, gl], (((1,), (1,)), ((), ())),
                                     preferred_element_type=jnp.float32)
@@ -427,10 +429,11 @@
     )(hidden, shard)
 
 
-Z_LAG = 4
+Z_LAG = 6
+BLOCK_GAP = 3
 CORE_LAG = 3
 BATCH = 4
-EARLY = 6
+EARLY = 4
 
 
 def fused_kernel(count, dims, len_ref, lenb_ref, bias_in, decay_in, skip_in, pdt_ref, dtt_ref,
@@ -536,15 +539,22 @@
     def ring(d, k, j, arrived=False):
         away = k if arrived else k - 1
         ref = piece(chip_at(r - away if d == 0 else r + away), j)
-        return remote(ref, ref, ring_s.at[d, k - 1, j], ring_r.at[d, k - 1, j],
+        return remote(ref, ref, ring_s.at[d, k - 1, j // 2], ring_r.at[d, k - 1, j],
                       seq=nxt if d == 0 else prv)
 
     def chip_of(u):
         return chip_at(r - u if u <= full else (r + (u - full) if u < far else r + half_ring))
 
-    def side(u, j, arrived=False):
-        ref = piece(chip_of(u), j, not arrived)
-        return remote(ref, ref, side_s.at[u, j], side_r.at[u, j], seq=partner)
+    def side(u, j):
+        ref = piece(chip_of(u), j)
+        return remote(ref, ref, side_s.at[u, j // 2], side_r.at[u, j // 2], seq=partner)
+
+    def both(where, kind, mine=True):
+        return (held_c if kind else held_b).at[where, pl.ds((core if mine else 1 - core) * 2, 2)]
+
+    def side_both(u, kind, arrived=False):
+        ref = both(chip_of(u), kind, not arrived)
+        return remote(ref, ref, side_s.at[u, kind], side_r.at[u, kind], seq=partner)
 
     def cross(kind, arrived=False):
         ref = held_c if kind else held_b
@@ -577,8 +587,7 @@
         acc[:, cols] = value if first else acc[:, cols] + value
 
     def mac(u, kind, first=False):
-        for j in (2 * kind, 2 * kind + 1):
-            side(u, j, True).wait_recv()
+        side_both(u, kind, True).wait_recv()
         q = chip_of(u)
         left = hid[:, pl.ds(pl.multiple_of(q * wide, wide), wide)]
         ref = held_c if kind else held_b
@@ -594,6 +603,9 @@
                     [left[:, s * wrows + o * LANES:s * wrows + (o + 1) * LANES] for s in range(4)], axis=1)
                 add(gw + o * LANES, jnp.dot(part, packs, preferred_element_type=jnp.float32), first)
 
+    def l_copy(back):
+        return remote(lout[back], lin[back], l_s.at[back], l_r.at[back], seq=partner)
+
     def exchange(back):
         pre, keep = kept[back][2:]
         for c in range(npair):
@@ -602,10 +614,10 @@
 
         def put(i, _):
             lout[back][i] = pre[nblocks, (1 - core) * half_pairs + i].astype(jnp.bfloat16)
-            remote(lout[back].at[i], lin[back].at[i], l_s.at[back, i], l_r.at[back, i], seq=partner).start()
             return 0
 
         lax.fori_loop(0, half_pairs, put, 0)
+        l_copy(back).start()
 
     def lead_core(back):
         return (core == 1) if back else (core == 0)
@@ -626,7 +638,7 @@
         return ref[pl.ds(i, 1), :]
 
     def x_copy(back, i):
-        return remote(xout[back].at[i], xin[back].at[i], c_s.at[back, i], c_r.at[back, i], seq=xpeer)
+        return remote(xout[back].at[i], xin[back].at[i], c_s.at[back], c_r.at[back, i], seq=xpeer)
 
     def kx_copy(back):
         return remote(kxo[back], kxi[back], k_s.at[2 + back], k_r.at[2 + back], seq=xpeer)
@@ -641,37 +653,47 @@
         def _():
             kx_copy(back).start()
 
-    def combine_part(back, start, stop):
+    def combine_part(back, send):
+        l_copy(back).wait_recv()
         pre = kept[back][2]
         sends = gives(back)
 
         def put(i, _):
             g = core * half_pairs + i
-            remote(lout[back].at[i], lin[back].at[i], l_s.at[back, i], l_r.at[back, i], seq=partner).wait_recv()
             lead = lead_core(back)
             total = (pre[nblocks, g] * jnp.where(lead, row(ksib[back], g), 1.0)
                      + lin[back][i].astype(jnp.float32) * jnp.where(lead, 1.0, row(kv[back], g)))
             xout[back][i] = total.astype(jnp.bfloat16)
-
-            @pl.when(sends)
-            def _():
-                x_copy(back, i).start()
+            if send:
+                @pl.when(sends)
+                def _():
+                    x_copy(back, i).start()
 
             return 0
 
-        lax.fori_loop(start, stop, put, 0)
+        lax.fori_loop(0, half_pairs, put, 0)
+
+    def x_sends(back, start, stop):
+        def put(i, _):
+            x_copy(back, i).start()
+            return 0
+
+        @pl.when(gives(back))
+        def _():
+            lax.fori_loop(start, stop, put, 0)
 
     def z_copy(back, i):
-        return remote(zout[back].at[i], zin[back].at[i], z_s.at[back, i], z_r.at[back, i],
+        return remote(zout[back].at[i], zin[back].at[i], z_s.at[back], z_r.at[back, i],
                       seq=me - 4 if back else me + 4)
 
-    def e_copy(back, i):
-        return remote(eout[back].at[i], ein[back].at[i], e_s.at[back, i], e_r.at[back, i], seq=partner)
+    def e_copy(back, k):
+        part = pl.ds(k * BATCH, BATCH)
+        return remote(eout[back].at[part], ein[back].at[part], e_s.at[back], e_r.at[back, k], seq=partner)
 
     def out_copy(back, k):
         cols = pl.ds(pl.multiple_of(k * BATCH * LANES, LANES), BATCH * LANES)
         src, dst = (gv, grad_hbm) if back else (xv, out_hbm)
-        return pltpu.make_async_copy(src.at[:, cols], dst.at[:, cols], o_sem.at[back, k])
+        return pltpu.make_async_copy(src.at[:, cols], dst.at[:, cols], o_sem.at[back])
 
     def finish(back, c0, states, i0):
         ins, fx, pre, keep = kept[back]
@@ -700,6 +722,14 @@
         g = core * half_pairs + i
         z_first, z_last = (zpos == nz - 1, zpos == 0) if back else (zpos == 0, zpos == nz - 1)
 
+        @pl.when((i == 0) & takes(back))
+        def _():
+            kx_copy(back).wait_recv()
+
+        @pl.when((i == 0) & jnp.logical_not(takes(back)))
+        def _():
+            kxi[back][...] = jnp.zeros_like(kxi[back])
+
         @pl.when(takes(back))
         def _():
             x_copy(back, i).wait_recv()
@@ -726,12 +756,15 @@
         l_lead = jnp.where(head, pre[nblocks, g], lin[back][i].astype(jnp.float32))
         after = k_lead * state + l_lead
         eout[back][i] = jnp.where(head, after, state).astype(jnp.bfloat16)
-        e_copy(back, i).start()
+
+        @pl.when(i % BATCH == BATCH - 1)
+        def _():
+            e_copy(back, i // BATCH).start()
+
         eown[back][i] = jnp.where(head, state, after).astype(jnp.bfloat16)
 
     def settle(back, i):
-        for k in range(BATCH):
-            e_copy(back, i + k).wait_recv()
+        e_copy(back, i // BATCH).wait_recv()
         finish(back, core * half_pairs + i, eown[back], i)
         finish(back, (1 - core) * half_pairs + i, ein[back], i)
 
@@ -739,7 +772,9 @@
         if back:
             in_block(True, dims, lenb_ref, gv, bp, cp, dtp, skip_ref, work_b, *kept[1][:2], span=(b, b + 1))
         else:
-            in_block(False, dims, len_ref, xv, cn, bn, dtn, skip_ref, work, *kept[0][:2])
+            at, g = b
+            in_block(False, dims, len_ref, xv, cn, bn, dtn, skip_ref, work, *kept[0][:2],
+                     span=(at, at + 1), only=g)
 
     for copy in b_loads:
         copy.wait()
@@ -753,6 +788,10 @@
     receive(1, 0, True)
     receive(1, 1)
     block(True, 1)
+    combine(1)
+    combine_part(1, False)
+    outer = (zpos == 0) | (zpos == nz - 1)
+    x_sends(1, 0, jnp.where(outer, 0, half_pairs))
     h_load.wait()
     mac(0, 0, True)
     c_next = [(k, second) for k in range(1, full + 1) for second in (False, True)][1:]
@@ -766,46 +805,44 @@
         for _ in range(2 if k == full else 1):
             step, second = c_next.pop(0)
             receive(step, 1, second)
+        if k == 2:
+            for u in (1, full + 1):
+                mac(u, 1)
     for u in (full, 2 * full):
         mac(u, 0)
     receive(full + 1, 0)
+    x_load.wait()
     mac(far, 0)
     at = gw
     bn[...] = acc[:, 0:gw].astype(jnp.bfloat16)
     dt_sum = acc[:, at:at + heads] + acc[:, at + LANES + heads:at + LANES + 2 * heads] + bias
     dtn[...] = jnp.maximum(dt_sum, 0.0) + jnp.log1p(jnp.exp(-jnp.abs(dt_sum)))
+
+    def forward_states(steps):
+        local_states(False, dims, len_ref, xv, bn, dtn, decay_ref, work, *kept[0][2:], part=steps)
+
+    forward_states((0,))
     while len(c_next) > 1:
         step, second = c_next.pop(0)
         receive(step, 1, second)
     early = jnp.where(zpos == 0, EARLY, half_pairs)
-    combine(1)
-    combine_part(1, 0, early)
-    x_load.wait()
-    local_states(False, dims, len_ref, xv, bn, dtn, decay_ref, work, *kept[0][2:])
+    x_sends(1, jnp.where(outer, 0, half_pairs), early)
+    forward_states(range(1, nblocks))
     exchange(0)
     for step, second in c_next:
         receive(step, 1, second)
-    for k in range(1, full):
+    for u in (2, full + 2):
+        mac(u, 1)
+    combine(0)
+    combine_part(0, True)
+    x_sends(1, early, half_pairs)
+    for k in range(3, full + 1):
         for u in (k, full + k):
             mac(u, 1)
-    combine(0)
-    combine_part(0, 0, half_pairs)
-    combine_part(1, early, half_pairs)
-    for u in (full, 2 * full):
-        mac(u, 1)
     receive(full + 1, 1)
     mac(far, 1)
     cn[...] = acc[:, gw + 2 * LANES:].astype(jnp.bfloat16)
-    block(False, 0)
-    for back in range(2):
-        @pl.when(takes(back))
-        def _(back=back):
-            kx_copy(back).wait_recv()
-
-        @pl.when(jnp.logical_not(takes(back)))
-        def _(back=back):
-            kxi[back][...] = jnp.zeros_like(kxi[back])
-
+    block_end = 1 + BLOCK_GAP * (groups * nblocks - 1)
 
     def tick(t, _):
         for back in range(2):
@@ -815,8 +852,16 @@
             def _(back=back, i=i):
                 relay(back, i)
 
+        for g in range(groups):
+            u = (t - 1) // BLOCK_GAP - g * nblocks
+
+            @pl.when(((t - 1) % BLOCK_GAP == 0) & (u >= 0) & (u < nblocks))
+            def _(u=u, g=g):
+                block(False, (u, g))
+
         for back in range(2):
-            late = t - ((nz - 1 - zpos) if back else zpos) * Z_LAG - CORE_LAG
+            lag = ((nz - 1 - zpos) if back else zpos) * Z_LAG + CORE_LAG
+            late = t - (lag if back else jnp.maximum(lag, block_end + 2 - BATCH))
 
             @pl.when((late >= 0) & (late < half_pairs) & (late % BATCH == BATCH - 1))
             def _(back=back, late=late):
@@ -824,18 +869,23 @@
 
         return 0
 
-    lax.fori_loop(0, half_pairs + CORE_LAG + (nz - 1) * Z_LAG, tick, 0)
+    last = max(half_pairs + CORE_LAG + (nz - 1) * Z_LAG, half_pairs + block_end + 2 - BATCH)
+    lax.fori_loop(0, last, tick, 0)
 
     for j in range(2):
         cross(j).wait_send()
     for k in range(1, half_ring + 1):
         for d in range(2):
-            for j in range(4):
-                if k <= full or j % 2 == d:
-                    ring(d, k, j).wait_send()
+            for kind in range(2):
+                if k > full:
+                    ring(d, k, 2 * kind + d).wait_send()
+                else:
+                    ref = both(chip, kind)
+                    remote(ref, ref, ring_s.at[d, k - 1, kind], ring_r.at[d, k - 1, 2 * kind],
+                           seq=partner).wait_send()
     for u in range(far + 1):
-        for j in range(4):
-            side(u, j).wait_send()
+        for kind in range(2):
+            side_both(u, kind).wait_send()
     for back in range(2):
         remote(kv[back], ksib[back], k_s.at[back], k_r.at[back], seq=partner).wait_send()
         given = gives(back)
@@ -844,24 +894,17 @@
         def _(back=back):
             kx_copy(back).wait_send()
 
-        def drain(i, _, back=back, given=given):
-            remote(lout[back].at[i], lin[back].at[i], l_s.at[back, i], l_r.at[back, i], seq=partner).wait_send()
-
-            @pl.when(given)
-            def _():
-                x_copy(back, i).wait_send()
-
-            e_copy(back, i).wait_send()
-
-            @pl.when(zpos != (0 if back else nz - 1))
-            def _():
-                z_copy(back, i).wait_send()
-
-            return 0
-
-        lax.fori_loop(0, half_pairs, drain, 0)
-        for k in range(npair // BATCH):
-            out_copy(back, k).wait()
+        @pl.when(given)
+        def _(back=back):
+            remote(xout[back], xin[back], c_s.at[back], c_r.at[back, 0], seq=xpeer).wait_send()
+
+        @pl.when(zpos != (0 if back else nz - 1))
+        def _(back=back):
+            remote(zout[back], zin[back], z_s.at[back], z_r.at[back, 0], seq=xpeer).wait_send()
+
+        l_copy(back).wait_send()
+        remote(eout[back], ein[back], e_s.at[back], e_r.at[back, 0], seq=partner).wait_send()
+        pltpu.make_async_copy(*((gv, grad_hbm) if back else (xv, out_hbm)), o_sem.at[back]).wait()
 
 
 def fused(hidden, values, seg_next, proj_bc, proj_dt, dt_bias, decay_rate, skip_gain,
@@ -902,10 +945,10 @@
             pltpu.VMEM((tokens, heads), f32), pltpu.VMEM((tokens, heads), f32),
             pltpu.VMEM((1, heads), f32), pltpu.VMEM((1, heads), f32),
             *work, *work, *kept, *kept, *box * 9, *gain * 2, *half_gain * 2,
-            dma((9,)), dma((2, steps, 4)), dma((2, steps, 4)), dma((n, 4)), dma((n, 4)),
-            dma((2,)), dma((2,)), dma((2, half_pairs)), dma((2, half_pairs)), dma((4,)), dma((4,)),
-            dma((2, half_pairs)), dma((2, half_pairs)), dma((2, half_pairs)), dma((2, half_pairs)),
-            dma((2, half_pairs)), dma((2, half_pairs)), dma((2, npair // BATCH)),
+            dma((9,)), dma((2, steps, 2)), dma((2, steps, 4)), dma((n, 2)), dma((n, 2)),
+            dma((2,)), dma((2,)), dma((2,)), dma((2,)), dma((4,)), dma((4,)),
+            dma((2,)), dma((2, half_pairs)), dma((2,)), dma((2, half_pairs)),
+            dma((2,)), dma((2, half_pairs // BATCH)), dma((2,)),
         ],
         compiler_params=pltpu.CompilerParams(
             collective_id=2, has_side_effects=True, vmem_limit_bytes=67_043_328),
@@ -918,12 +961,12 @@
         out_shape=[jax.ShapeDtypeStruct(values.shape, bf16)] * 2,
         in_specs=[hbm] * 2,
         out_specs=[hbm] * 2,
-        scratch_shapes=[chunk, chunk, dma((2, HAND_PARTS)), dma((2, HAND_PARTS))],
+        scratch_shapes=[chunk, chunk, dma((2, HAND_PARTS)), dma((2,))],
         name="hand_over",
     )(*staged)
 
 
-HAND_PARTS = 8
+HAND_PARTS = 4
 
 
 def hand_over(a_in, b_in, a_out, b_out, a_buf, b_buf, in_sem, out_sem):
@@ -933,14 +976,14 @@
         rows = pl.ds(p * part, part)
         for k, (src, buf, dst) in enumerate(((a_in, a_buf, a_out), (b_in, b_buf, b_out))):
             reads.append(pltpu.make_async_copy(src.at[rows, :], buf.at[rows, :], in_sem.at[k, p]))
-            writes.append(pltpu.make_async_copy(buf.at[rows, :], dst.at[rows, :], out_sem.at[k, p]))
+            writes.append(pltpu.make_async_copy(buf.at[rows, :], dst.at[rows, :], out_sem.at[k]))
     for copy in reads:
         copy.start()
     for read, write in zip(reads, writes):
         read.wait()
         write.start()
-    for copy in writes:
-        copy.wait()
+    for k, (buf, dst) in enumerate(((a_buf, a_out), (b_buf, b_out))):
+        pltpu.make_async_copy(buf, dst, out_sem.at[k]).wait()
 
 
 def body(

time: 93.1 us -> 85.2 us (0.915); the launches traced: 91.6 us -> 85 us
  Pallas kernels: 90.8 us -> 84.2 us
    pallas_call x1, Pallas kernels: 87 us -> 80.7 us  [fused(): pl.pallas_call(functools.partial(fused_kernel, count, dims), out_shape=[j...]
where the time goes in v3:
time: 85.2 us; the launch traced here: 85 us
  Pallas kernels  84.2 us (99%)
    pallas_call x1, Pallas kernels, fused(): pl.pallas_call(functools.partial(fused_kernel, count, dims), out_shape=[j...  80.7 us
    pallas_call x1, Pallas kernels, fused(): pl.pallas_call(hand_over, out_shape=[jax.ShapeDtypeStruct(values.shape, b...  3.52 us

profile of v3, /device:TPU:0, one launch (start us, length us, event | category | flops | bytes accessed | tf_op | source)
XLA Modules:
  0.0 85.0 jit_solution(15704463259613961411)
XLA Ops:
  0.6 80.7 %fused.1 = (bf16[256,4096]{1,0:T(8,128)(2,1)}, bf16[256,4096]{1,0:T(8,128)(2,1)}) custom-call(s32[4]{0:T(128)} %len_ref.1, s32[4]{0:T(128)} %lenb_ref.1, f32[1,128]{1,0:T(1,128)} %bitcast.5, f32[1,128]{1,0:T(1,128)} %bitcast.6, f32[1,128]{1,0:T(1,128)} %bitcast.7, bf16[256,128]{1,0:T(8,128)(2,1)} %pdt_ref.1, f32[64,256]{1,0:T(8,128)} %bitcast.4, ...), custom_call_target="tpu_custom_call" | custom-call | tf_op jit(solution)/shard_map/fused/pallas_call | solution.py:933
  81.3 3.5 %hand_over.1 = (bf16[256,4096]{1,0:T(8,128)(2,1)}, bf16[256,4096]{1,0:T(8,128)(2,1)}) custom-call(bf16[256,4096]{1,0:T(8,128)(2,1)} %get-tuple-element.4.a_in, bf16[256,4096]{1,0:T(8,128)(2,1)} %get-tuple-element.5.b_in), custom_call_target="tpu_custom_call" | custom-call | tf_op jit(solution)/shard_map/hand_over/pallas_call | solution.py:959

commit v4 on v3

--- a/solution.py
+++ b/solution.py
@@ -433,7 +433,7 @@
 BLOCK_GAP = 3
 CORE_LAG = 3
 BATCH = 4
-EARLY = 4
+EARLY = 0
 
 
 def fused_kernel(count, dims, len_ref, lenb_ref, bias_in, decay_in, skip_in, pdt_ref, dtt_ref,

time: 85.2 us -> 84.2 us (0.988)
  Pallas kernels: 84.2 us -> 82.8 us
    pallas_call x1, Pallas kernels: 80.7 us -> 79.3 us  [fused(): pl.pallas_call(functools.partial(fused_kernel, count, dims), out_shape=[j...]
where the time goes in v4:
time: 84.2 us; the launch traced here: 83.6 us
  Pallas kernels  82.8 us (98%)
    pallas_call x1, Pallas kernels, fused(): pl.pallas_call(functools.partial(fused_kernel, count, dims), out_shape=[j...  79.3 us
    pallas_call x1, Pallas kernels, fused(): pl.pallas_call(hand_over, out_shape=[jax.ShapeDtypeStruct(values.shape, b...  3.52 us

profile of v4, /device:TPU:0, one launch (start us, length us, event | category | flops | bytes accessed | tf_op | source)
XLA Modules:
  0.0 83.6 jit_solution(11358451658912794142)
XLA Ops:
  0.6 79.3 %fused.1 = (bf16[256,4096]{1,0:T(8,128)(2,1)}, bf16[256,4096]{1,0:T(8,128)(2,1)}) custom-call(s32[4]{0:T(128)} %len_ref.1, s32[4]{0:T(128)} %lenb_ref.1, f32[1,128]{1,0:T(1,128)} %bitcast.5, f32[1,128]{1,0:T(1,128)} %bitcast.6, f32[1,128]{1,0:T(1,128)} %bitcast.7, bf16[256,128]{1,0:T(8,128)(2,1)} %pdt_ref.1, f32[64,256]{1,0:T(8,128)} %bitcast.4, ...), custom_call_target="tpu_custom_call" | custom-call | tf_op jit(solution)/shard_map/fused/pallas_call | solution.py:933
  80.0 3.5 %hand_over.1 = (bf16[256,4096]{1,0:T(8,128)(2,1)}, bf16[256,4096]{1,0:T(8,128)(2,1)}) custom-call(bf16[256,4096]{1,0:T(8,128)(2,1)} %get-tuple-element.4.a_in, bf16[256,4096]{1,0:T(8,128)(2,1)} %get-tuple-element.5.b_in), custom_call_target="tpu_custom_call" | custom-call | tf_op jit(solution)/shard_map/hand_over/pallas_call | solution.py:959
